TPU v7x, 32 devices: a 4x4x1 block of a 4x4x8 slice. The times are simulated.
32 devices in a mesh: dp: 1 (over z), tp: 4 (over y), wg: 8 (over x, core).
Axes of the slice: x: 4, y: 4, z: 1, core: 2. Of those that a mesh axis runs over, the one named last changes fastest.
The devices are a block of a 4x4x8 slice.
Arguments:
- tokens: bfloat16 [1024, 2560], P(('dp', 'wg'))
- gain_attn: float32 [2560], P('wg')
- gain_mlp: float32 [2560], P('wg')
- w_qkv: bfloat16 [2560, 3, 32, 80], P('wg', None, 'tp')
- w_rel: bfloat16 [2560, 32, 80], P('wg', 'tp')
- w_out: bfloat16 [32, 80, 2560], P('tp', None, 'wg')
- w_up: bfloat16 [2560, 10240], P('wg', 'tp')
- w_down: bfloat16 [10240, 2560], P('tp', 'wg')
- bias_u: float32 [32, 80], P('tp')
- bias_v: float32 [32, 80], P('tp')
- rel_table: bfloat16 [16, 2560], replicated
- k_cache: bfloat16 [1024, 32, 16, 80], P(('dp', 'wg'), 'tp')
- v_cache: bfloat16 [1024, 32, 16, 80], P(('dp', 'wg'), 'tp')
- positions: int32 [1024], P(('dp', 'wg'))
Outputs:
- output 1: bfloat16 [1024, 2560], P(('dp', 'wg'))
- output 2: bfloat16 [1024, 32, 80], P(('dp', 'wg'), 'tp')
- output 3: bfloat16 [1024, 32, 80], P(('dp', 'wg'), 'tp')
All inputs are finite; a program needn't handle non-finite values.
Results may differ from a plain program's by a relative error of at most 0.0133234.
Values are sent between devices in bfloat16 or wider.
A program may use at most 768 MiB of HBM per device.

v0:
```python
import jax
import jax.numpy as jnp
from jax import lax
from jax.sharding import PartitionSpec as P

NORM_EPS = 1e-6


def rms_norm(row_vals, gain_vec):
    vals_f32 = row_vals.astype(jnp.float32)
    mean_sq = jnp.mean(vals_f32 * vals_f32, axis=-1, keepdims=True)
    return (vals_f32 * lax.rsqrt(mean_sq + NORM_EPS) * gain_vec).astype(jnp.bfloat16)


def cache_attention(q_u, q_v, k_new, v_new, k_cache, v_cache, positions, rel_proj):
    cache_len = k_cache.shape[2]
    score_scale = q_u.shape[-1] ** -0.5
    key_steps = jnp.arange(cache_len)
    is_self = (key_steps[None, :] == positions[:, None])[:, None, :]
    is_valid = (key_steps[None, :] <= positions[:, None])[:, None, :]
    content = jnp.einsum("bhe,bhje->bhj", q_u, k_cache, preferred_element_type=jnp.float32)
    self_score = jnp.einsum("bhe,bhe->bh", q_u, k_new, preferred_element_type=jnp.float32)
    content = jnp.where(is_self, self_score[:, :, None], content)
    rel_all = jnp.einsum("bhe,rhe->bhr", q_v, rel_proj, preferred_element_type=jnp.float32)
    rel_index = jnp.clip(positions[:, None] - key_steps[None, :], 0, cache_len - 1)
    rel_scores = jnp.take_along_axis(rel_all, jnp.broadcast_to(rel_index[:, None, :], rel_all.shape), axis=2)
    scores = jnp.where(is_valid, (content + rel_scores) * score_scale, -1e30)
    attn_probs = jax.nn.softmax(scores, axis=-1).astype(jnp.bfloat16)
    zero_probs = jnp.zeros_like(attn_probs)
    self_prob = jnp.sum(jnp.where(is_self, attn_probs, zero_probs), axis=-1, dtype=jnp.float32)
    cache_probs = jnp.where(is_self, zero_probs, attn_probs)
    attn_out = jnp.einsum("bhj,bhje->bhe", cache_probs, v_cache, preferred_element_type=jnp.float32)
    attn_out = attn_out + self_prob[:, :, None] * v_new.astype(jnp.float32)
    return attn_out.astype(jnp.bfloat16)


def solution(mesh):
    tok_axes = ("dp", "wg")
    in_specs = (P(tok_axes, None), P("wg"), P("wg"), P("wg", None, "tp", None), P("wg", "tp", None), P("tp", None, "wg"), P("wg", "tp"), P("tp", "wg"), P("tp", None), P("tp", None), P(None, None), P(tok_axes, "tp", None, None), P(tok_axes, "tp", None, None), P(tok_axes))
    out_specs = (P(tok_axes, None), P(tok_axes, "tp", None), P(tok_axes, "tp", None))

    def device_step(tokens, gain_attn, gain_mlp, w_qkv, w_rel, w_out, w_up, w_down, bias_u, bias_v, rel_table, k_cache, v_cache, positions):
        gain_attn_full = lax.all_gather(gain_attn, "wg", axis=0, tiled=True)
        gain_mlp_full = lax.all_gather(gain_mlp, "wg", axis=0, tiled=True)
        qkv_full = lax.all_gather(w_qkv, "wg", axis=0, tiled=True)
        rel_full = lax.all_gather(w_rel, "wg", axis=0, tiled=True)
        out_full = lax.all_gather(w_out, "wg", axis=2, tiled=True)
        up_full = lax.all_gather(w_up, "wg", axis=0, tiled=True)
        down_full = lax.all_gather(w_down, "wg", axis=1, tiled=True)
        normed = rms_norm(tokens, gain_attn_full)
        qkv_heads = jnp.einsum("td,dshe->tshe", normed, qkv_full, preferred_element_type=jnp.float32).astype(jnp.bfloat16)
        q_heads = qkv_heads[:, 0]
        k_new = qkv_heads[:, 1]
        v_new = qkv_heads[:, 2]
        rel_proj = jnp.einsum("rd,dhe->rhe", rel_table, rel_full, preferred_element_type=jnp.float32).astype(jnp.bfloat16)
        q_u = (q_heads.astype(jnp.float32) + bias_u).astype(jnp.bfloat16)
        q_v = (q_heads.astype(jnp.float32) + bias_v).astype(jnp.bfloat16)
        attn_out = cache_attention(q_u, q_v, k_new, v_new, k_cache, v_cache, positions, rel_proj)
        attn_part = jnp.einsum("the,hed->td", attn_out, out_full, preferred_element_type=jnp.float32).astype(jnp.bfloat16)
        attn_sum = lax.psum(attn_part, "tp")
        resid = tokens.astype(jnp.float32) + attn_sum.astype(jnp.float32)
        normed_mlp = rms_norm(resid, gain_mlp_full)
        hidden = jax.nn.gelu(jnp.dot(normed_mlp, up_full, preferred_element_type=jnp.float32), approximate=True).astype(jnp.bfloat16)
        mlp_part = jnp.dot(hidden, down_full, preferred_element_type=jnp.float32).astype(jnp.bfloat16)
        mlp_sum = lax.psum(mlp_part, "tp")
        layer_out = (resid + mlp_sum.astype(jnp.float32)).astype(jnp.bfloat16)
        return layer_out, k_new, v_new

    return jax.shard_map(device_step, mesh=mesh, in_specs=in_specs, out_specs=out_specs, check_vma=False)
```

profile of v0, /device:TPU:96, one launch (start us, length us, event | category | flops | bytes accessed | tf_op | source)
XLA Modules:
  0.0 517.7 jit_solution(7520975215183889622)
XLA Ops:
  7.2 0.0 copy-start
  7.2 0.1 all-gather.6.cloned.1.call-start
  7.3 0.0 copy-start.19
  7.3 0.0 copy-start.14
  7.3 0.0 copy-start.15
  7.3 0.0 copy-start.2
  7.3 4.0 copy.26
  11.4 0.1 all-gather.6.cloned.1.call-update
  11.4 0.1 all-gather.8.cloned.1.call-start
  11.5 1.2 copy.31
  12.7 0.1 all-gather.8.cloned.1.call-update
  12.8 0.1 all-gather.10.cloned.1.call-start
  12.9 1.2 copy.35
  14.1 0.1 all-gather.10.cloned.1.call-update
  14.2 0.1 all-reduce.6.cloned.1.call-start
  14.3 0.7 copy.28
  15.0 0.7 copy.29
  15.7 0.7 copy.30
  16.5 0.2 copy.33
  16.7 0.2 reshape.90
  16.9 0.7 copy.24
  17.6 0.7 copy.25
  18.3 0.0 copy-done.19
  18.3 0.6 dynamic-slice
  19.6 0.3 dynamic-update-slice
  19.9 0.3 dynamic-update-slice.1
  20.1 27.8 %all-reduce.2 = (f32[2560]{0:T(1024)S(1)}, f32[2560]{0:T(1024)}) all-reduce(f32[2560]{0:T(1024)S(1)} %dynamic-update-slice, f32[2560]{0:T(1024)S(1)} %dynamic-update-slice.1), channel_id=1, replica_groups=mesh['dp'=1,'tp'=4,'wg'=8] {'wg'}, use_global_device_ids=true, to_apply=%add | all-reduce | flops 5120 | bytes 40960
  48.0 0.2 fusion.12
  48.2 44.4 %all-gather.6.cloned.1.call-done = bf16[2560,3,8,80]{3,2,1,0:T(8,128)(2,1)} async-done(((bf16[320,3,8,80]{3,2,1,0:T(8,128)(2,1)}), bf16[2560,3,8,80]{3,2,1,0:T(8,128)(2,1)}) %all-gather.6.cloned.1.call-update) | async-done | bytes 9830416 | tf_op jit(solution)/shard_map/all_gather | solution.py:45
  92.6 19.1 %copy.27 = bf16[2560,3,8,80]{0,3,2,1:T(8,128)(2,1)} copy(bf16[2560,3,8,80]{3,2,1,0:T(8,128)(2,1)} %all-gather.6.cloned.1.call-done) | data formatting | bytes 19660800 | tf_op jit(solution)/shard_map/all_gather | solution.py:45
  111.7 5.4 %fusion.33 = f32[128,1920]{0,1:S(1)} fusion(bf16[2560,1920]{0,1:T(8,128)(2,1)} %bitcast.37, bf16[128,2560]{1,0:T(8,128)(2,1)S(1)} %copy-done.2, f32[2560]{0:T(1024)S(1)} %get-tuple-element.3, f32[128]{0:T(128)S(1)} %add_rsqrt_fusion.1), kind=kOutput, calls=%fused_computation.39 | convolution fusion | flops 1259601920 | bytes 11479552
  117.1 0.1 convert_element_type.61
  117.2 11.0 %all-gather.8.cloned.1.call-done = bf16[2560,8,80]{2,1,0:T(8,128)(2,1)} async-done(((bf16[320,8,80]{2,1,0:T(8,128)(2,1)}), bf16[2560,8,80]{2,1,0:T(8,128)(2,1)}) %all-gather.8.cloned.1.call-update) | async-done | bytes 3276816 | tf_op jit(solution)/shard_map/all_gather | solution.py:46
  128.2 3.4 convolution_bitcast_fusion
  131.7 131.2 %gather_fusion = f32[16384]{0:T(1024)S(1)} fusion(f32[128,8,16]{0,2,1:T(8,128)S(1)} %convolution_bitcast_fusion, s32[16384]{0:T(1024)S(1)} %reshape.90), kind=kCustom, calls=%fused_computation | custom fusion | bytes 327680 | tf_op jit(solution)/shard_map/jit(take_along_axis)/gather | solution.py:26
  262.9 1.0 reshape.93
  263.9 1.7 multiply_reduce_fusion.3
  265.6 0.9 multiply_reduce_fusion.1
  266.5 0.0 copy-start.6
  266.5 1.0 copy.48
  267.5 0.1 copy.41
  267.6 1.9 select_convert_fusion
  269.5 0.2 convert_reduce_fusion
  269.8 0.2 copy.56
  270.0 0.9 slice_bitcast_fusion
  271.0 0.0 copy-start.10
  271.0 0.6 multiply_reduce_fusion
  271.6 0.0 copy-start.3
  271.6 0.0 all-gather.10.cloned.1.call-done
  271.7 5.3 %fusion.9 = bf16[128,2560]{1,0:T(8,128)(2,1)} fusion(bf16[8,80,2560]{1,0,2:T(8,128)(2,1)} %all-gather.10.cloned.1.call-done, f32[128,8,80]{0,2,1:T(8,128)S(1)} %multiply_reduce_fusion, bf16[128,8,80]{0,2,1:T(8,128)(2,1)S(1)} %slice_bitcast_fusion, f32[128,8]{0,1:T(8,128)S(1)} %copy.34), kind=kOutput, calls=%fused_computation.10 | convolution fusion | flops 420085760 | bytes 4427776 | tf_op jit(solution)/shard_map/the,hed->td/dot_general | solution.py:59
  276.9 0.1 all-reduce.6.cloned.1.call-update
  277.0 0.1 all-gather.12.cloned.1.call-start
  277.1 0.6 all-gather.12.cloned.1.call-update
  277.6 0.1 all-gather.14.cloned.1.call-start
  277.7 0.6 all-gather.14.cloned.1.call-update
  278.3 0.2 all-reduce.8.cloned.1.call-start
  278.5 37.3 %all-reduce.6.cloned.1.call-done = bf16[128,2560]{1,0:T(8,128)(2,1)} async-done(((bf16[128,2560]{1,0:T(8,128)(2,1)}), bf16[128,2560]{1,0:T(8,128)(2,1)}) %all-reduce.6.cloned.1.call-update) | async-done | bytes 655376 | tf_op jit(solution)/shard_map/psum | solution.py:60
  315.8 1.4 multiply_reduce_fusion.2
  317.2 67.6 %all-gather.12.cloned.1.call-done = bf16[2560,2560]{1,0:T(8,128)(2,1)} async-done(((bf16[320,2560]{1,0:T(8,128)(2,1)}), bf16[2560,2560]{1,0:T(8,128)(2,1)}) %all-gather.12.cloned.1.call-update) | async-done | bytes 13107216 | tf_op jit(solution)/shard_map/all_gather | solution.py:48
  384.8 68.9 %all-gather.14.cloned.1.call-done = bf16[2560,2560]{0,1:T(8,128)(2,1)} async-done(((bf16[2560,320]{0,1:T(8,128)(2,1)}), bf16[2560,2560]{0,1:T(8,128)(2,1)}) %all-gather.14.cloned.1.call-update) | async-done | bytes 13107216 | tf_op jit(solution)/shard_map/all_gather | solution.py:49
  453.7 15.8 %convolution_convert_fusion = bf16[128,2560]{1,0:T(8,128)(2,1)} fusion(bf16[2560,2560]{0,1:T(8,128)(2,1)} %all-gather.14.cloned.1.call-done, bf16[2560,2560]{1,0:T(8,128)(2,1)} %all-gather.12.cloned.1.call-done, bf16[128,2560]{1,0:T(8,128)(2,1)} %all-reduce.6.cloned.1.call-done, bf16[128,2560]{1,0:T(8,128)(2,1)S(1)} %copy-done.3, f32[2560]{0:T(1024)S(1)} %copy-done.17, ...), kind=kOutput, calls=%fused_computation.11 | convolution fusion | flops 3360686080 | bytes 28191232 | tf_op jit(solution)/shard_map/dot_general | solution.py:64
  469.5 0.1 all-reduce.8.cloned.1.call-update
  469.6 39.1 %all-reduce.8.cloned.1.call-done = bf16[128,2560]{1,0:T(8,128)(2,1)} async-done(((bf16[128,2560]{1,0:T(8,128)(2,1)}), bf16[128,2560]{1,0:T(8,128)(2,1)}) %all-reduce.8.cloned.1.call-update) | async-done | bytes 655376 | tf_op jit(solution)/shard_map/psum | solution.py:65
  508.7 2.2 add_convert_fusion
  (39 shorter events, 0.2 us)
Async XLA Ops:
  7.2 121.0 %copy-start = (bf16[16,2560]{1,0:T(8,128)(2,1)S(1)}, bf16[16,2560]{1,0:T(8,128)(2,1)}, u32[]{:S(2)}) copy-start(bf16[16,2560]{1,0:T(8,128)(2,1)} %param.24) | copy-start | bytes 245764
  7.2 4.3 copy-start.8
  7.2 5.7 %copy-start.9 = (bf16[8,80,320]{2,1,0:T(8,128)(2,1)S(1)}, bf16[8,80,320]{2,1,0:T(8,128)(2,1)}, u32[]{:S(2)}) copy-start(bf16[8,80,320]{2,1,0:T(8,128)(2,1)} %param.19) | copy-start | bytes 1228804
  7.2 7.0 %copy-start.16 = (s32[128]{0:T(128)S(1)}, s32[128]{0:T(128)}, u32[]{:S(2)}) copy-start(s32[128]{0:T(128)} %param.27) | copy-start | bytes 1540
  7.2 85.4 %all-gather.6.cloned.1.call-start = ((), (), s32[]{:S(2)}) async-start(), calls=%async_computation | async-start | bytes 17694720 | tf_op jit(solution)/shard_map/all_gather | solution.py:45
  7.3 11.0 %copy-start.19 = (u32[32]{0:T(128)S(1)}, u32[32]{0:T(128)}, u32[]{:S(2)}) copy-start(u32[32]{0:T(128)} %constant.64) | copy-start | bytes 388
  7.3 12.3 %copy-start.14 = (f32[320]{0:T(512)S(1)}, f32[320]{0:T(512)}, u32[]{:S(2)}) copy-start(f32[320]{0:T(512)} %param.15) | copy-start | bytes 3844
  7.3 12.5 %copy-start.15 = (f32[320]{0:T(512)S(1)}, f32[320]{0:T(512)}, u32[]{:S(2)}) copy-start(f32[320]{0:T(512)} %param.16) | copy-start | bytes 3844
  7.3 40.7 %copy-start.2 = (bf16[128,2560]{1,0:T(8,128)(2,1)S(1)}, bf16[128,2560]{1,0:T(8,128)(2,1)}, u32[]{:S(2)}) copy-start(bf16[128,2560]{1,0:T(8,128)(2,1)} %param.14) | copy-start | bytes 1966084
  11.4 116.8 %all-gather.8.cloned.1.call-start = ((), (), s32[]{:S(2)}) async-start(), calls=%async_computation.1 | async-start | bytes 5898240 | tf_op jit(solution)/shard_map/all_gather | solution.py:46
  12.8 258.9 %all-gather.10.cloned.1.call-start = ((), (), s32[]{:S(2)}) async-start(), calls=%async_computation.2 | async-start | bytes 5898240 | tf_op jit(solution)/shard_map/all_gather | solution.py:47
  14.2 301.6 %all-reduce.6.cloned.1.call-start = ((), (), s32[]{:S(2)}) async-start(), calls=%async_computation.3 | async-start | bytes 1310720 | tf_op jit(solution)/shard_map/psum | solution.py:60
  111.7 16.6 %copy-start.18 = (f32[8,80]{1,0:T(8,128)S(1)}, f32[8,80]{1,0:T(8,128)}, u32[]{:S(2)}) copy-start(f32[8,80]{1,0:T(8,128)} %param.23) | copy-start | bytes 7684
  117.2 145.7 %copy-start.7 = (bf16[128,3,8,80]{0,3,2,1:T(8,128)(2,1)}, bf16[128,3,8,80]{0,3,2,1:T(8,128)(2,1)S(1)}, u32[]{:S(2)}) copy-start(bf16[128,3,8,80]{0,3,2,1:T(8,128)(2,1)S(1)} %convert_element_type.61) | copy-start | bytes 1474564
  131.6 132.3 %copy-start.13 = (f32[8,80]{1,0:T(8,128)S(1)}, f32[8,80]{1,0:T(8,128)}, u32[]{:S(2)}) copy-start(f32[8,80]{1,0:T(8,128)} %param.22) | copy-start | bytes 7684
  131.6 134.0 %copy-start.5 = (bf16[128,8,16,80]{0,3,2,1:T(8,128)(2,1)S(1)}, bf16[128,8,16,80]{0,3,2,1:T(8,128)(2,1)}, u32[]{:S(2)}) copy-start(bf16[128,8,16,80]{0,3,2,1:T(8,128)(2,1)} %param.25) | copy-start | bytes 7864324
  131.6 136.0 %copy-start.11 = (s32[128,16]{1,0:T(8,128)S(1)}, s32[128,16]{1,0:T(8,128)}, u32[]{:S(2)}) copy-start(s32[128,16]{1,0:T(8,128)} %copy.29) | copy-start | bytes 24580
  131.6 136.0 %copy-start.12 = (pred[128,16]{1,0:T(8,128)(4,1)S(1)}, pred[128,16]{1,0:T(8,128)(4,1)}, u32[]{:S(2)}) copy-start(pred[128,16]{1,0:T(8,128)(4,1)} %copy.24) | copy-start | bytes 6148
  266.5 4.5 copy-start.6
  271.0 5.9 %copy-start.10 = (bf16[128,8,80]{0,2,1:T(8,128)(2,1)}, bf16[128,8,80]{0,2,1:T(8,128)(2,1)S(1)}, u32[]{:S(2)}) copy-start(bf16[128,8,80]{0,2,1:T(8,128)(2,1)S(1)} %slice_bitcast_fusion) | copy-start | bytes 491524
  271.6 44.2 %copy-start.3 = (bf16[128,2560]{1,0:T(8,128)(2,1)S(1)}, bf16[128,2560]{1,0:T(8,128)(2,1)}, u32[]{:S(2)}) copy-start(bf16[128,2560]{1,0:T(8,128)(2,1)} %param.14) | copy-start | bytes 1966084
  271.6 182.0 %copy-start.17 = (f32[2560]{0:T(1024)S(1)}, f32[2560]{0:T(1024)}, u32[]{:S(2)}) copy-start(f32[2560]{0:T(1024)} %get-tuple-element.4) | copy-start | bytes 30724
  277.0 107.8 %all-gather.12.cloned.1.call-start = ((), (), s32[]{:S(2)}) async-start(), calls=%async_computation.4 | async-start | bytes 14745600 | tf_op jit(solution)/shard_map/all_gather | solution.py:48
  277.6 176.0 %all-gather.14.cloned.1.call-start = ((), (), s32[]{:S(2)}) async-start(), calls=%async_computation.5 | async-start | bytes 14745600 | tf_op jit(solution)/shard_map/all_gather | solution.py:49
  278.3 230.4 %all-reduce.8.cloned.1.call-start = ((), (), s32[]{:S(2)}) async-start(), calls=%async_computation.6 | async-start | bytes 1310720 | tf_op jit(solution)/shard_map/psum | solution.py:65
  453.7 55.0 %copy-start.4 = (bf16[128,2560]{1,0:T(8,128)(2,1)S(1)}, bf16[128,2560]{1,0:T(8,128)(2,1)}, u32[]{:S(2)}) copy-start(bf16[128,2560]{1,0:T(8,128)(2,1)} %all-reduce.6.cloned.1.call-done) | copy-start | bytes 1966084
  453.7 57.2 %copy-start.1 = (bf16[16,2560]{1,0:T(8,128)(2,1)S(1)}, bf16[16,2560]{1,0:T(8,128)(2,1)}, u32[]{:S(2)}) copy-start(bf16[16,2560]{1,0:T(8,128)(2,1)} %param.24) | copy-start | bytes 245764
Sparse Core Ops, SparseCore 0:
  11.5 80.9 all-gather.5
  94.2 34.0 all-gather.7
  130.4 33.6 all-gather.9
  277.1 38.6 all-reduce.5
  317.2 67.4 all-gather.11
  386.2 67.4 all-gather.13
  469.7 38.9 all-reduce.7
where the time goes:
time: 519 us; the launch traced here: 518 us
  waiting for transfers between devices  270 us (52%)
  local copies, waits for them, and re-layouts  165 us (32%)
  matrix products  30 us (6%)
  blocking collectives  27.8 us (5%)
  between operations  15.1 us (3%)
  other arithmetic  9.21 us (2%)
    gather x4, local copies, waits for them, and re-layouts, cache_attention(): jnp.take_along_axis(rel_all, jnp.broadcast_to(rel_index[:, None, :], rel_...  133 us
    all_gather x1, waiting for transfers between devices, device_step(): down_full = lax.all_gather(w_down, 'wg', axis=1, tiled=True)  68.9 us
    all_gather x1, waiting for transfers between devices, device_step(): up_full = lax.all_gather(w_up, 'wg', axis=0, tiled=True)  67.6 us
    all_gather x1, waiting for transfers between devices, device_step(): qkv_full = lax.all_gather(w_qkv, 'wg', axis=0, tiled=True)  44.4 us
    psum x1, waiting for transfers between devices, device_step(): mlp_sum = lax.psum(mlp_part, 'tp')  39.1 us
    psum x1, waiting for transfers between devices, device_step(): attn_sum = lax.psum(attn_part, 'tp')  37.3 us
    unnamed x1, blocking collectives  27.8 us
    all_gather x1, local copies, waits for them, and re-layouts, device_step(): qkv_full = lax.all_gather(w_qkv, 'wg', axis=0, tiled=True)  19.1 us
  transfers between devices with their start and end apart: 7, of which 6 were waited for; matrix products, arithmetic and copies ran while one was open for 34% of the time, Pallas kernels for 0%

commit v1 on v0

v1 whole, which is shorter than its diff:
```python
import functools
import math

import jax
import jax.numpy as jnp
from jax import lax
from jax.experimental import pallas as pl
from jax.experimental.pallas import tpu as pltpu
from jax.sharding import PartitionSpec as P

MESH = pl.DeviceIdType.MESH
NORM_EPS = 1e-6
BF16 = jnp.bfloat16
F32 = jnp.float32
NT = (((1,), (1,)), ((), ()))
NN = (((1,), (0,)), ((), ()))
N_REMOTE = 160
N_LOCAL = 32


def dot(a, b, dims):
    return lax.dot_general(a, b, dims, preferred_element_type=F32)


def layer_kernel(nx, ny, tok_ref, ga_ref, gm_ref, wqkv_ref, wrel_ref, wout_ref, wup_ref, wdn_ref, bu_ref, bv_ref, relt_ref, kc_ref, vc_ref, pos_ref,
                 y_ref, kn_ref, vn_ref,
                 xall, nall, gall, gmx, wq_land, wq, qst, qin, kc, vc, wrel, rsend, rland, s_ref, p_ref, o_t, oall, wo_land, wo,
                 st1, in1, hbuf, st_s, st_r, mall, wup, zall, wdn, st2, in2, yst, yfull,
                 ss, rs, ls):
    w = lax.axis_index("wg")
    x, c, y = w // 2, w % 2, lax.axis_index("tp")
    rows, d_model = tok_ref.shape
    ds = ga_ref.shape[1]
    dx = 2 * ds
    n_heads, n_slots, hd, _ = kc_ref.shape
    hx = n_heads // nx
    fx = wup_ref.shape[1] // nx
    qr = rows // ny
    hw = n_heads * hd

    def dev(xx, cc, yy):
        return {"wg": 2 * xx + cc, "tp": yy}

    def xp(i):
        return lax.rem(x + i, nx)

    def yp(i):
        return lax.rem(y + i, ny)

    sib = dev(x, 1 - c, y)
    counter = [0, 0]
    pending = []

    def new():
        counter[0] += 1
        return counter[0] - 1

    def send(src, dst, to, i):
        cp = pltpu.make_async_remote_copy(src_ref=src, dst_ref=dst, send_sem=ss.at[i], recv_sem=rs.at[i], device_id=to, device_id_type=MESH)
        cp.start()
        pending.append(cp)

    def arrived(dst, i):
        pltpu.make_async_remote_copy(src_ref=dst, dst_ref=dst, send_sem=ss.at[i], recv_sem=rs.at[i], device_id=sib, device_id_type=MESH).wait_recv()

    def local(src, dst):
        cp = pltpu.make_async_copy(src, dst, ls.at[counter[1]])
        counter[1] += 1
        cp.start()
        return cp

    def xlane(ref_cols, xx):
        return pl.ds(pl.multiple_of(xx * ref_cols, 128), ref_cols)

    def qrow(yy):
        return pl.ds(pl.multiple_of(yy * qr, qr), qr)

    xs, ys = range(1, nx), range(1, ny)

    c_x = local(tok_ref, xall.at[x])
    c_wq = local(wqkv_ref.at[:, pl.ds(x * hx, hx)], wq_land.at[w])
    c_rel = local(wrel_ref, wrel)
    c_ga = local(ga_ref, gall.at[w])
    c_gm = local(gm_ref, gmx.at[c])
    c_k = local(kc_ref, kc)
    c_v = local(vc_ref, vc)
    c_wo = local(wout_ref, wo_land.at[c])
    c_up = local(wup_ref.at[:, xlane(fx, x)], wup.at[w])
    c_dn = local(wdn_ref, wdn.at[c])

    barrier = pltpu.get_barrier_semaphore()
    peers = [dev(xp(i), c, y) for i in xs] + [dev(x, c, yp(i)) for i in ys] + [sib] + [dev(xp(i), 1 - c, y) for i in xs]
    for peer in peers:
        pl.semaphore_signal(barrier, inc=1, device_id=peer, device_id_type=MESH)
    pl.semaphore_wait(barrier, len(peers))

    i_tx = {i: new() for i in xs}
    for i in xs:
        send(tok_ref.at[qrow(y)], xall.at[x, qrow(y)], dev(xp(i), c, y), i_tx[i])
    i_ga = {}
    for i in range(nx):
        for f in range(2):
            if i or f:
                i_ga[i, f] = new()
                to = dev(xp(i), lax.rem(c + f, 2), y)
                send(ga_ref, gall.at[w], to, i_ga[i, f])
    i_gm = new()
    send(gm_ref, gmx.at[c], sib, i_gm)
    i_wx = {i: new() for i in xs}
    for i in xs:
        send(wqkv_ref.at[:, pl.ds(xp(i) * hx, hx)], wq_land.at[w], dev(xp(i), c, y), i_wx[i])
    i_ws = {i: new() for i in range(nx)}
    send(wqkv_ref.at[:, pl.ds(x * hx, hx)], wq_land.at[w], sib, i_ws[0])
    c_rel.wait()
    tab = relt_ref[:, xlane(dx, x)]
    tab = jnp.where(c == 0, tab[:, :ds], tab[:, ds:])
    rsend[...] = dot(tab, wrel[...], NT)
    rland[w] = rsend[...]
    i_rel = {}
    for i in range(nx):
        for f in range(2):
            if i or f:
                i_rel[i, f] = new()
                send(rsend, rland.at[w], dev(xp(i), lax.rem(c + f, 2), y), i_rel[i, f])
    i_ty = {(i, k): new() for i in xs for k in ys}
    for i in xs:
        src = lax.rem(x + nx - i, nx)
        blk = xall.at[src, qrow(y)]
        arrived(blk, i_tx[i])
        for k in ys:
            send(blk, blk, dev(x, c, yp(k)), i_ty[i, k])
    i_wo, i_dn = new(), new()
    send(wout_ref, wo_land.at[c], sib, i_wo)
    send(wdn_ref, wdn.at[c], sib, i_dn)
    for i in xs:
        blk = wq_land.at[2 * lax.rem(x + nx - i, nx) + c]
        arrived(blk, i_wx[i])
        send(blk, blk, sib, i_ws[i])
    for i in range(nx):
        for f in range(2):
            if i or f:
                arrived(gall.at[2 * lax.rem(x + nx - i, nx) + lax.rem(c + f, 2)], i_ga[i, f])
    c_ga.wait()
    gain = jnp.concatenate([gall[j] for j in range(2 * nx)], axis=1)
    c_x.wait()
    for i in xs:
        for k in ys:
            arrived(xall.at[lax.rem(x + nx - i, nx), qrow(lax.rem(y + ny - k, ny))], i_ty[i, k])
    blk_rows = 32

    def norm_block(r, carry):
        g = r // (rows // blk_rows)
        b = pl.ds(pl.multiple_of(lax.rem(r, rows // blk_rows) * blk_rows, blk_rows), blk_rows)
        v = xall[g, b, :].astype(F32)
        ms = jnp.mean(v * v, axis=-1, keepdims=True)
        nall[g, b, :] = (v * lax.rsqrt(ms + NORM_EPS) * gain).astype(BF16)
        return carry

    lax.fori_loop(0, nx * rows // blk_rows, norm_block, 0)
    c_wq.wait()
    for i in range(nx):
        arrived(wq_land.at[2 * lax.rem(x + nx - i, nx) + 1 - c], i_ws[i])
    for j in range(nx):
        for s in range(3):
            for e in range(hx):
                pair = jnp.concatenate([wq_land[2 * j, s, e], wq_land[2 * j + 1, s, e]], axis=1)
                wq[(s * hx + e) * hd:(s * hx + e + 1) * hd, j * dx:(j + 1) * dx] = pair
    i_q = {i: new() for i in xs}
    for g in range(nx):
        res = dot(wq[...], nall[g], NT).astype(BF16)
        qst[g] = res.reshape(3, hx, hd, rows)
    for i in xs:
        send(qst.at[xp(i)], qin.at[x], dev(xp(i), c, y), i_q[i])
    qin[x] = qst[x]
    i_ux = {i: new() for i in xs}
    i_us = {i: new() for i in range(nx)}
    send(wup_ref.at[:, xlane(fx, x)], wup.at[w], sib, i_us[0])
    for i in range(nx):
        for f in range(2):
            if i or f:
                arrived(rland.at[2 * lax.rem(x + nx - i, nx) + lax.rem(c + f, 2)], i_rel[i, f])
    rel = rland[0]
    for j in range(1, 2 * nx):
        rel = rel + rland[j]
    rel = rel.astype(BF16).astype(F32)
    rel = jnp.broadcast_to(rel[:, None, :], (n_slots, n_heads, hw)).reshape(n_slots * n_heads, hw)
    col = lax.broadcasted_iota(jnp.int32, rel.shape, 1)
    row_head = lax.rem(lax.broadcasted_iota(jnp.int32, rel.shape, 0), n_heads)
    keep = (col >= row_head * hd) & (col < row_head * hd + hd)
    rel_diag = jnp.where(keep, rel, 0.0).astype(BF16)

    for i in xs:
        arrived(qin.at[lax.rem(x + nx - i, nx)], i_q[i])
    outs = []
    for j in range(nx):
        outs.append(local(qin.at[j, 1], kn_ref.at[j * hx:(j + 1) * hx]))
        outs.append(local(qin.at[j, 2], vn_ref.at[j * hx:(j + 1) * hx]))
    pos = pos_ref[...]
    bu_t, bv_t = bu_ref[...].T, bv_ref[...].T
    scale = 1.0 / math.sqrt(hd)
    c_k.wait()
    selfs, qvs = [], []
    for h in range(n_heads):
        q = qin[h // hx, 0, h % hx].astype(F32)
        qu = (q + bu_t[:, h:h + 1]).astype(BF16).astype(F32)
        qvs.append((q + bv_t[:, h:h + 1]).astype(BF16))
        selfs.append(jnp.sum(qu * qin[h // hx, 1, h % hx].astype(F32), axis=0, keepdims=True))
        for j in range(n_slots):
            s_ref[j, h:h + 1, :] = jnp.sum(kc[h, j].astype(F32) * qu, axis=0, keepdims=True)
    self_score = jnp.concatenate(selfs, axis=0)
    rel_all = dot(rel_diag, jnp.concatenate(qvs, axis=0), NN)
    rel_all = [rel_all[r * n_heads:(r + 1) * n_heads] for r in range(n_slots)][::-1]
    shift = n_slots - 1 - pos
    bit = 1
    while bit < n_slots:
        take = (shift // bit) % 2 == 1
        rel_all = [jnp.where(take, rel_all[j + bit], rel_all[j]) if j + bit < n_slots else rel_all[j] for j in range(n_slots)]
        bit *= 2
    sc = []
    for j in range(n_slots):
        content = jnp.where(pos == j, self_score, s_ref[j])
        sc.append(jnp.where(pos >= j, (content + rel_all[j]) * scale, -1e30))
    top = functools.reduce(jnp.maximum, sc)
    ex = [jnp.exp(v - top) for v in sc]
    tot = functools.reduce(jnp.add, ex)
    probs = [(v / tot).astype(BF16).astype(F32) for v in ex]
    self_prob = functools.reduce(jnp.add, [jnp.where(pos == j, probs[j], 0.0) for j in range(n_slots)])
    for j in range(n_slots):
        p_ref[j] = jnp.where(pos == j, 0.0, probs[j])
    p_ref[n_slots] = self_prob
    c_v.wait()
    for h in range(n_heads):
        acc = p_ref[n_slots, h:h + 1, :] * qin[h // hx, 2, h % hx].astype(F32)
        for j in range(n_slots):
            acc = acc + p_ref[j, h:h + 1, :] * vc[h, j].astype(F32)
        o_t[h * hd:(h + 1) * hd, :] = acc
    oall[x] = o_t[...].T.astype(BF16)
    i_o = {i: new() for i in xs}
    for i in xs:
        send(oall.at[x], oall.at[x], dev(xp(i), c, y), i_o[i])
    for i in xs:
        send(wup_ref.at[:, xlane(fx, xp(i))], wup.at[w], dev(xp(i), c, y), i_ux[i])
    c_wo.wait()
    arrived(wo_land.at[1 - c], i_wo)
    wo[...] = jnp.concatenate([wo_land[0], wo_land[1]], axis=1)
    for i in xs:
        arrived(oall.at[lax.rem(x + nx - i, nx)], i_o[i])
    for g in range(nx):
        part = dot(oall[g], wo[...], NN).astype(BF16)
        for k in range(ny):
            st1[k, g * qr:(g + 1) * qr, :] = part[k * qr:(k + 1) * qr]
    i_r1 = {i: new() for i in ys}
    for i in ys:
        send(st1.at[yp(i)], in1.at[y], dev(x, c, yp(i)), i_r1[i])
    in1[y] = st1[y]
    c_gm.wait()
    arrived(gmx.at[1 - c], i_gm)
    gain_m = jnp.concatenate([gmx[0], gmx[1]], axis=1)
    for i in ys:
        arrived(in1.at[lax.rem(y + ny - i, ny)], i_r1[i])
    acc = in1[0].astype(F32)
    for k in range(1, ny):
        acc = acc + in1[k].astype(F32)
    for g in range(nx):
        hbuf[g * qr:(g + 1) * qr, :] = xall[g, qrow(y), xlane(dx, x)].astype(F32) + acc[g * qr:(g + 1) * qr]
    h = hbuf[...]
    sq = jnp.sum(h * h, axis=1, keepdims=True)
    sq = jnp.broadcast_to(sq, (rows, rows)).T[:8]
    st_s[...] = sq
    st_r[x] = sq
    i_s = {i: new() for i in xs}
    for i in xs:
        send(st_s, st_r.at[x], dev(xp(i), c, y), i_s[i])
    for i in xs:
        arrived(st_r.at[lax.rem(x + nx - i, nx)], i_s[i])
    tot = st_r[0]
    for j in range(1, nx):
        tot = tot + st_r[j]
    rstd = lax.rsqrt(tot * (1.0 / d_model) + NORM_EPS)
    rstd = jnp.broadcast_to(rstd[0:1], (rows, rows)).T[:, 0:1]
    mall[y, :, xlane(dx, x)] = (hbuf[...] * rstd * gain_m).astype(BF16)
    half = rows // 2
    lo, hi = pl.ds(0, half), pl.ds(half, half)

    def mpiece(yy, xx, part):
        return mall.at[yy, part, xlane(dx, xx)]

    i_m = {(p, a): new() for p in "xy" for a in range(1, 4)}
    i_mf = {(p, a, b): new() for p in "xy" for a in range(4) for b in range(1, 4)}
    for i in xs:
        send(mpiece(y, x, lo), mpiece(y, x, lo), dev(xp(i), c, y), i_m["x", i])
    for i in ys:
        send(mpiece(y, x, hi), mpiece(y, x, hi), dev(x, c, yp(i)), i_m["y", i])
    for k in ys:
        send(mpiece(y, x, lo), mpiece(y, x, lo), dev(x, c, yp(k)), i_mf["x", 0, k])
    for k in xs:
        send(mpiece(y, x, hi), mpiece(y, x, hi), dev(xp(k), c, y), i_mf["y", 0, k])
    for i in range(1, 4):
        a = lax.rem(x + nx - i, nx)
        arrived(mpiece(y, a, lo), i_m["x", i])
        for k in ys:
            send(mpiece(y, a, lo), mpiece(y, a, lo), dev(x, c, yp(k)), i_mf["x", i, k])
        b = lax.rem(y + ny - i, ny)
        arrived(mpiece(b, x, hi), i_m["y", i])
        for k in xs:
            send(mpiece(b, x, hi), mpiece(b, x, hi), dev(xp(k), c, y), i_mf["y", i, k])
    for i in xs:
        blk = wup.at[2 * lax.rem(x + nx - i, nx) + c]
        arrived(blk, i_ux[i])
        send(blk, blk, sib, i_us[i])
    for i in range(4):
        for k in range(1, 4):
            arrived(mpiece(lax.rem(y + ny - k, ny), lax.rem(x + nx - i, nx), lo), i_mf["x", i, k])
            arrived(mpiece(lax.rem(y + ny - i, ny), lax.rem(x + nx - k, nx), hi), i_mf["y", i, k])
    c_up.wait()
    for i in range(nx):
        arrived(wup.at[2 * lax.rem(x + nx - i, nx) + 1 - c], i_us[i])
    up = wup[...].reshape(d_model, fx)
    i_z = {(k, i): new() for k in range(ny) for i in xs}
    order = [lax.rem(y + 1 + k, ny) for k in range(ny)]
    for k, q in enumerate(order):
        z = dot(mall[q], up, NN)
        zall[q, :, xlane(fx, x)] = jax.nn.gelu(z, approximate=True).astype(BF16)
        for i in xs:
            send(zall.at[q, :, xlane(fx, x)], zall.at[q, :, xlane(fx, x)], dev(xp(i), c, y), i_z[k, i])
    c_dn.wait()
    arrived(wdn.at[1 - c], i_dn)
    dn = wdn[...].reshape(dx, zall.shape[2])
    i_r2 = {k: new() for k in ys}
    for k, q in enumerate(order):
        for i in xs:
            arrived(zall.at[q, :, xlane(fx, lax.rem(x + nx - i, nx))], i_z[k, i])
        part = dot(zall[q], dn, NT).astype(BF16)
        if k < ny - 1:
            st2[k] = part
            send(st2.at[k], in2.at[y], dev(x, c, q), i_r2[k + 1])
        else:
            in2[y] = part
    for i in ys:
        arrived(in2.at[lax.rem(y + ny - i, ny)], i_r2[i])
    acc = in2[0].astype(F32)
    for k in range(1, ny):
        acc = acc + in2[k].astype(F32)
    yst[...] = (hbuf[...] + acc).astype(BF16).reshape(nx, qr, dx)
    i_yx = {i: new() for i in xs}
    for i in xs:
        send(yst.at[xp(i)], yfull.at[y, :, xlane(dx, x)], dev(xp(i), c, y), i_yx[i])
    yfull[y, :, xlane(dx, x)] = yst[x]
    i_yy = {(i, k): new() for i in range(nx) for k in ys}
    for i in range(nx):
        blk = yfull.at[y, :, xlane(dx, lax.rem(x + nx - i, nx))]
        if i:
            arrived(blk, i_yx[i])
        for k in ys:
            send(blk, blk, dev(x, c, yp(k)), i_yy[i, k])
    for i in range(nx):
        for k in ys:
            arrived(yfull.at[lax.rem(y + ny - k, ny), :, xlane(dx, lax.rem(x + nx - i, nx))], i_yy[i, k])
    outs.append(local(yfull, y_ref))
    for cp in pending:
        cp.wait_send()
    for cp in outs:
        cp.wait()
    assert counter[0] <= N_REMOTE and counter[1] <= N_LOCAL


def solution(mesh):
    nx, ny = mesh.shape["wg"] // 2, mesh.shape["tp"]
    tok_axes = ("dp", "wg")
    in_specs = (P(tok_axes, None), P("wg"), P("wg"), P("wg", None, "tp", None), P("wg", "tp", None), P("tp", None, "wg"), P("wg", "tp"), P("tp", "wg"), P("tp", None), P("tp", None), P(None, None), P(tok_axes, "tp", None, None), P(tok_axes, "tp", None, None), P(tok_axes))
    out_specs = (P(tok_axes, None), P(tok_axes, "tp", None), P(tok_axes, "tp", None))

    def device_step(tokens, gain_attn, gain_mlp, w_qkv, w_rel, w_out, w_up, w_down, bias_u, bias_v, rel_table, k_cache, v_cache, positions):
        rows, d_model = tokens.shape
        ds = gain_attn.shape[0]
        dx = 2 * ds
        _, n_heads, n_slots, hd = k_cache.shape
        hx = n_heads // nx
        hw = n_heads * hd
        ff = w_up.shape[1]
        fx = ff // nx
        qr = rows // ny
        any_spec = pl.BlockSpec(memory_space=pl.ANY)
        vmem_spec = pl.BlockSpec(memory_space=pltpu.VMEM)
        vm = pltpu.VMEM
        scratch = [
            vm((nx, rows, d_model), BF16),
            vm((nx, rows, d_model), BF16),
            vm((2 * nx, 1, ds), F32),
            vm((2, 1, ds), F32),
            vm((2 * nx, 3, hx, hd, ds), BF16),
            vm((3 * hx * hd, d_model), BF16),
            vm((nx, 3, hx, hd, rows), BF16),
            vm((nx, 3, hx, hd, rows), BF16),
            vm((n_heads, n_slots, hd, rows), BF16),
            vm((n_heads, n_slots, hd, rows), BF16),
            vm((hw, ds), BF16),
            vm((n_slots, hw), F32),
            vm((2 * nx, n_slots, hw), F32),
            vm((n_slots, n_heads, rows), F32),
            vm((n_slots + 1, n_heads, rows), F32),
            vm((hw, rows), F32),
            vm((nx, rows, hw), BF16),
            vm((2, hw, ds), BF16),
            vm((hw, dx), BF16),
            vm((ny, rows, dx), BF16),
            vm((ny, rows, dx), BF16),
            vm((rows, dx), F32),
            vm((8, rows), F32),
            vm((nx, 8, rows), F32),
            vm((ny, rows, d_model), BF16),
            vm((2 * nx, ds, fx), BF16),
            vm((ny, rows, ff), BF16),
            vm((2, ds, ff), BF16),
            vm((ny - 1, rows, dx), BF16),
            vm((ny, rows, dx), BF16),
            vm((nx, qr, dx), BF16),
            vm((ny, qr, d_model), BF16),
            pltpu.SemaphoreType.DMA((N_REMOTE,)),
            pltpu.SemaphoreType.DMA((N_REMOTE,)),
            pltpu.SemaphoreType.DMA((N_LOCAL,)),
        ]
        y, kn, vn = pl.pallas_call(
            functools.partial(layer_kernel, nx, ny),
            out_shape=(
                jax.ShapeDtypeStruct((ny, qr, d_model), BF16),
                jax.ShapeDtypeStruct((n_heads, hd, rows), BF16),
                jax.ShapeDtypeStruct((n_heads, hd, rows), BF16),
            ),
            in_specs=[any_spec, vmem_spec, vmem_spec, any_spec, any_spec, any_spec, any_spec, any_spec, vmem_spec, vmem_spec, vmem_spec, any_spec, any_spec, vmem_spec],
            out_specs=(any_spec, any_spec, any_spec),
            scratch_shapes=scratch,
            compiler_params=pltpu.CompilerParams(collective_id=0, has_side_effects=True, vmem_limit_bytes=60 * 2**20),
        )(
            tokens, gain_attn[None, :], gain_mlp[None, :], w_qkv.transpose(1, 2, 3, 0), w_rel.transpose(1, 2, 0).reshape(hw, ds), w_out.reshape(hw, ds),
            w_up, w_down.T, bias_u, bias_v, rel_table, k_cache.transpose(1, 2, 3, 0), v_cache.transpose(1, 2, 3, 0), positions[None, :],
        )
        return y.reshape(rows, d_model), kn.transpose(2, 0, 1), vn.transpose(2, 0, 1)

    return jax.shard_map(device_step, mesh=mesh, in_specs=in_specs, out_specs=out_specs, check_vma=False)
```

time: 519 us -> 146 us (0.28)
  waiting for transfers between devices: 270 us -> 0 us
  local copies, waits for them, and re-layouts: 165 us -> 6.76 us
  Pallas kernels: 0 us -> 138 us
  matrix products: 30 us -> 0 us
  blocking collectives: 27.8 us -> 0 us
  between operations: 15.1 us -> 0.65 us
  other arithmetic: 9.21 us -> 0 us
    all_gather x5 -> x0, waiting for transfers between devices: 192 us -> none  [the longest x1 68.9 us: device_step(): down_full = lax.all_gather(w_down, 'wg', axis=1, tiled=True)]
    pallas_call x0 -> x1, Pallas kernels: none -> 138 us  [device_step(): pl.pallas_call(functools.partial(layer_kernel, nx, ny), out_shape=(jax.Sh...]
    gather x4 -> x0, local copies, waits for them, and re-layouts: 133 us -> none  [cache_attention(): jnp.take_along_axis(rel_all, jnp.broadcast_to(rel_index[:, None, :], rel_...]
    psum x2 -> x0, waiting for transfers between devices: 76.4 us -> none  [the longest x1 39.1 us: device_step(): mlp_sum = lax.psum(mlp_part, 'tp')]
    unnamed x1 -> x0, blocking collectives: 27.8 us -> none
    dot_general x3 -> x0, matrix products: 24.5 us -> none  [the longest x1 15.8 us: device_step(): jnp.dot(hidden, down_full, preferred_element_type=jnp.float32)]
    all_gather x1 -> x0, local copies, waits for them, and re-layouts: 19.1 us -> none  [device_step(): qkv_full = lax.all_gather(w_qkv, 'wg', axis=0, tiled=True)]
    unnamed x1 -> x0, matrix products: 5.44 us -> none
  transfers between devices with their start and end apart: 7 -> 0, of which waited for: 6 -> 0; matrix products, arithmetic and copies ran while one was open for 34% -> 0% of each run, Pallas kernels for 0% -> 0%
where the time goes in v1:
time: 146 us
  Pallas kernels  138 us (95%)
  local copies, waits for them, and re-layouts  6.76 us (5%)
    pallas_call x1, Pallas kernels, device_step(): pl.pallas_call(functools.partial(layer_kernel, nx, ny), out_shape=(jax.Sh...  138 us
    unnamed x5, local copies, waits for them, and re-layouts  4.27 us

profile of v1, /device:TPU:96, one launch (start us, length us, event | category | flops | bytes accessed | tf_op | source)
XLA Modules:
  0.0 145.6 jit_solution(738418323619866477)
XLA Ops:
  0.6 1.2 broadcast_in_dim.9.ga_ref
  1.9 1.2 broadcast_in_dim.10.gm_ref
  3.1 138.1 %shard_map.157 = (bf16[4,32,2560]{2,1,0:T(8,128)(2,1)}, bf16[8,80,128]{2,1,0:T(8,128)(2,1)}, bf16[8,80,128]{2,1,0:T(8,128)(2,1)}) custom-call(bf16[128,2560]{1,0:T(8,128)(2,1)} %tok_ref.1, f32[1,320]{1,0:T(1,128)} %broadcast_in_dim.9.ga_ref, f32[1,320]{1,0:T(1,128)} %broadcast_in_dim.10.gm_ref, bf16[3,8,80,320]{3,2,1,0:T(8,128)(2,1)} %bitcast.15, ...), custom_call_target="tpu_custom_call" | custom-call | tf_op jit(solution)/shard_map/pallas_call | solution.py:423
  141.3 0.0 copy-start
  141.3 2.0 %copy.20 = bf16[128,2560]{1,0:T(8,128)(2,1)} copy(bf16[128,2560]{1,0:T(8,128)(2,1)} %bitcast.16) | data formatting | bytes 1310720
  143.3 1.6 %copy.21 = bf16[128,8,80]{0,2,1:T(8,128)(2,1)} copy(bf16[128,8,80]{0,2,1:T(8,128)(2,1)} %bitcast.20) | data formatting | bytes 327680
  144.9 0.0 copy-done
  144.9 0.7 copy.22
Async XLA Ops:
  141.3 3.6 %copy-start = (bf16[8,80,128]{2,1,0:T(8,128)(2,1)S(1)}, bf16[8,80,128]{2,1,0:T(8,128)(2,1)}, u32[]{:S(2)}) copy-start(bf16[8,80,128]{2,1,0:T(8,128)(2,1)} %get-tuple-element.8) | copy-start | bytes 491524

commit v2 on v1

v2 whole, which is shorter than its diff:
```python
import functools
import math

import jax
import jax.numpy as jnp
from jax import lax
from jax.experimental import pallas as pl
from jax.experimental.pallas import tpu as pltpu
from jax.sharding import PartitionSpec as P

MESH = pl.DeviceIdType.MESH
NORM_EPS = 1e-6
BF16 = jnp.bfloat16
F32 = jnp.float32
NT = (((1,), (1,)), ((), ()))
NN = (((1,), (0,)), ((), ()))
N_REMOTE = 224
N_LOCAL = 32
UP_PARTS = (0, 96, 128, 272, 320)


def dot(a, b, dims):
    return lax.dot_general(a, b, dims, preferred_element_type=F32)


def layer_kernel(nx, ny, tok_ref, ga_ref, gm_ref, wqkv_ref, wrel_ref, wout_ref, wup_ref, wdn_ref, bu_ref, bv_ref, relt_ref, kc_ref, vc_ref, pos_ref,
                 y_ref, kn_ref, vn_ref,
                 xall, nall, gst, gall, gain, wq_land, wpk, wq, qst, qin, kc, vc, wrel, rsend, rsib, rland, rfull, rel_diag, s_ref, p_ref, o_t, oall, wo_land, wo,
                 st1, in1, hbuf, st_s, st_r, mall, wup, zall, wdn, st2, in2, yst, yfull,
                 ss, rs, ls):
    w = lax.axis_index("wg")
    x, c, y = w // 2, w % 2, lax.axis_index("tp")
    rows, d_model = tok_ref.shape
    ds = ga_ref.shape[0]
    dx = 2 * ds
    n_heads, n_slots, hd, _ = kc_ref.shape
    hx = n_heads // nx
    fx = wup_ref.shape[1] // nx
    qr = rows // ny
    hw = n_heads * hd
    ff = wup_ref.shape[1]

    def dev(xx, cc, yy):
        return {"wg": 2 * xx + cc, "tp": yy}

    def xp(i):
        return lax.rem(x + i, nx)

    def yp(i):
        return lax.rem(y + i, ny)

    sib = dev(x, 1 - c, y)
    right, left = dev(xp(1), c, y), dev(xp(nx - 1), c, y)
    above, below = dev(x, c, yp(1)), dev(x, c, yp(ny - 1))
    xof = {"S": x, "L": xp(nx - 1), "R": xp(1), "O": xp(2)}
    yof = {"S": y, "D": yp(ny - 1), "U": yp(1), "O": yp(2)}
    ids = {}
    pending = []
    n_local = [0]

    def nid(key):
        return ids.setdefault(key, len(ids))

    def send(src, dst, to, key):
        i = nid(key)
        cp = pltpu.make_async_remote_copy(src_ref=src, dst_ref=dst, send_sem=ss.at[i], recv_sem=rs.at[i], device_id=to, device_id_type=MESH)
        cp.start()
        pending.append(cp)

    def arrived(dst, key):
        i = nid(key)
        pltpu.make_async_remote_copy(src_ref=dst, dst_ref=dst, send_sem=ss.at[i], recv_sem=rs.at[i], device_id=sib, device_id_type=MESH).wait_recv()

    def local(src, dst):
        cp = pltpu.make_async_copy(src, dst, ls.at[n_local[0]])
        n_local[0] += 1
        cp.start()
        return cp

    def lanes(size, k):
        return pl.ds(pl.multiple_of(k * size, 128), size)

    def rowsl(start, size):
        return pl.ds(pl.multiple_of(start, 16), size)

    def x_start(name, unit, own=None):
        own = own or (lambda h: unit(x, h))
        for h, to, frm in ((0, right, "L"), (1, left, "R"), (1, right, "L"), (0, left, "R")):
            send(own(h), unit(x, h), to, (name, frm, h))

    def x_relay(name, unit, frm):
        h, to = (0, right) if frm == "L" else (1, left)
        arrived(unit(xof[frm], h), (name, frm, h))
        send(unit(xof[frm], h), unit(xof[frm], h), to, (name, "O", h))

    def x_wait(name, unit, frm, h):
        arrived(unit(xof[frm], h), (name, frm, h))

    def y_send(name, unit, px, h):
        blk = unit(xof[px], y, h)
        send(blk, blk, above, (name, px, "D", h))
        send(blk, blk, below, (name, px, "U", h))

    def y_relay(name, unit, px, frm):
        h, to = (0, above) if frm == "D" else (1, below)
        blk = unit(xof[px], yof[frm], h)
        arrived(blk, (name, px, frm, h))
        send(blk, blk, to, (name, px, "O", h))

    def y_wait(name, unit, px, frm, h):
        arrived(unit(xof[px], yof[frm], h), (name, px, frm, h))

    c_wq = local(wqkv_ref.at[:, :, c], wq_land.at[c])
    c_rel = local(wrel_ref, wrel)
    c_x = local(tok_ref, xall.at[x])
    c_k = local(kc_ref, kc)
    c_v = local(vc_ref, vc)
    c_wo = local(wout_ref, wo_land.at[c])
    c_up = local(wup_ref.at[:, lanes(fx, x)], wup.at[w])
    c_dn = local(wdn_ref, wdn.at[c])
    gst[0:1, :] = ga_ref[...].reshape(1, ds)
    gst[1:2, :] = gm_ref[...].reshape(1, ds)
    gall[w] = gst[...]

    barrier = pltpu.get_barrier_semaphore()
    peers = [dev(xp(i), c, y) for i in range(1, nx)] + [dev(x, c, yp(i)) for i in range(1, ny)] + [sib]
    for peer in peers:
        pl.semaphore_signal(barrier, inc=1, device_id=peer, device_id_type=MESH)
    pl.semaphore_wait(barrier, len(peers))

    hq = qr // 2

    def tok_unit(xx, yy, h):
        return xall.at[xx, rowsl(yy * qr + h * hq, hq)]

    def tok_x(xx, h):
        return tok_unit(xx, y, h)

    x_start("tx", tok_x, lambda h: tok_ref.at[rowsl(y * qr + h * hq, hq)])
    send(wqkv_ref.at[:, :, 1 - c], wq_land.at[c], sib, "wqs")
    send(gst, gall.at[w], sib, ("g", 0))
    for i in range(1, nx):
        send(gst, gall.at[w], dev(xp(i), c, y), ("g", i))
    c_rel.wait()
    tab = relt_ref[:, lanes(dx, x)]
    tab = jnp.where(c == 0, tab[:, :ds], tab[:, ds:])
    part = dot(tab, wrel[...], NT)
    hs = n_slots // 2
    rsend[...] = part.reshape(2, hs, hw)
    send(rsend.at[1 - c], rsib, sib, "r0")
    x_relay("tx", tok_x, "L")
    y_send("ty", tok_unit, "L", 0)
    x_relay("tx", tok_x, "R")
    y_send("ty", tok_unit, "R", 1)
    c_wq.wait()
    arrived(wq_land.at[1 - c], "wqs")
    for s in range(3):
        for j in range(nx):
            wpk[s, j] = jnp.concatenate([wq_land[0, s, j], wq_land[1, s, j]], axis=1)
    for i, key in ((1, "L"), (nx - 1, "R"), (2, "O")):
        send(wpk.at[:, xp(i)], wq.at[:, c, :, lanes(dx, x)], dev(xp(i), c, y), ("wx", key))
    wq[:, c, :, lanes(dx, x)] = wpk[:, x]
    send(wpk.at[:, x], wq.at[:, c, :, lanes(dx, x)], sib, ("ws", "S"))
    arrived(rsib, "r0")
    rland[x] = rsend[c] + rsib[...]
    for i, key in ((1, "L"), (nx - 1, "R"), (2, "O")):
        send(rland.at[x], rland.at[x], dev(xp(i), c, y), ("r1", key))
    for frm, h in (("L", 1), ("R", 0), ("O", 0), ("O", 1)):
        x_wait("tx", tok_x, frm, h)
        y_send("ty", tok_unit, frm, h)

    def up_send(p):
        r0, r1 = UP_PARTS[p], UP_PARTS[p + 1]
        for i, key in ((1, "L"), (nx - 1, "R"), (2, "O")):
            send(wup_ref.at[r0:r1, lanes(fx, xp(i))], wup.at[w, r0:r1], dev(xp(i), c, y), ("ux", p, key))

    def up_relay(p):
        r0, r1 = UP_PARTS[p], UP_PARTS[p + 1]
        for key in "LRO":
            blk = wup.at[2 * xof[key] + c, r0:r1]
            arrived(blk, ("ux", p, key))
            send(blk, blk, sib, ("us", p, key))

    up_send(0)
    send(wout_ref, wo_land.at[c], sib, "wo")
    send(wdn_ref, wdn.at[c], sib, "dn")
    send(wup_ref.at[:, lanes(fx, x)], wup.at[w], sib, "uown")
    for i in range(1, nx):
        blk = gall.at[2 * lax.rem(x + nx - i, nx) + c]
        arrived(blk, ("g", i))
        send(blk, blk, sib, ("gs", i))
    arrived(gall.at[2 * x + 1 - c], ("g", 0))
    for i in range(1, nx):
        arrived(gall.at[2 * lax.rem(x + nx - i, nx) + 1 - c], ("gs", i))
    gain[...] = jnp.concatenate([gall[j, 0:1, :] for j in range(2 * nx)], axis=1)
    blk_rows = 32

    def norm_group(g):
        def norm_block(r, carry):
            b = pl.ds(pl.multiple_of(r * blk_rows, blk_rows), blk_rows)
            v = xall[g, b, :].astype(F32)
            ms = jnp.mean(v * v, axis=-1, keepdims=True)
            nall[g, b, :] = (v * lax.rsqrt(ms + NORM_EPS) * gain[...]).astype(BF16)
            return carry

        lax.fori_loop(0, rows // blk_rows, norm_block, 0)

    c_x.wait()
    norm_group(x)
    for px, frm in (("L", "D"), ("R", "U"), ("L", "U"), ("R", "D"), ("O", "D"), ("O", "U")):
        y_relay("ty", tok_unit, px, frm)
    for key in "LRO":
        blk = wq.at[:, c, :, lanes(dx, xof[key])]
        arrived(blk, ("wx", key))
        send(blk, blk, sib, ("ws", key))
    for px in "LRO":
        for frm, h in (("D", 1), ("U", 0), ("O", 0), ("O", 1)):
            y_wait("ty", tok_unit, px, frm, h)
        norm_group(xof[px])
    for key in "SLRO":
        arrived(wq.at[:, 1 - c, :, lanes(dx, xof[key])], ("ws", key))
    wqv = wq[...].reshape(3 * hx * hd, d_model)
    for i, key in ((2, "O"), (1, "L"), (nx - 1, "R"), (0, "S")):
        g = xp(i)
        res = dot(wqv, nall[g], NT).astype(BF16).reshape(3, hx, hd, rows)
        if i:
            qst[i - 1] = res
            send(qst.at[i - 1], qin.at[x], dev(g, c, y), ("q", key))
        else:
            qin[x] = res
    up_send(1)
    for key in "LRO":
        arrived(rland.at[xof[key]], ("r1", key))
    rel = rland[0]
    for j in range(1, nx):
        rel = rel + rland[j]
    rfull[c] = rel
    send(rfull.at[c], rfull.at[c], sib, "r2")
    up_relay(0)
    arrived(rfull.at[1 - c], "r2")
    rel = rfull[...].reshape(n_slots, hw).astype(BF16).astype(F32)
    rel = jnp.broadcast_to(rel[:, None, :], (n_slots, n_heads, hw)).reshape(n_slots * n_heads, hw)
    col = lax.broadcasted_iota(jnp.int32, rel.shape, 1)
    row_head = lax.rem(lax.broadcasted_iota(jnp.int32, rel.shape, 0), n_heads)
    keep = (col >= row_head * hd) & (col < row_head * hd + hd)
    rel_diag[...] = jnp.where(keep, rel, 0.0).astype(BF16)
    c_k.wait()
    for key in "LRO":
        arrived(qin.at[xof[key]], ("q", key))
    outs = []
    for j in range(nx):
        outs.append(local(qin.at[j, 1], kn_ref.at[j * hx:(j + 1) * hx]))
        outs.append(local(qin.at[j, 2], vn_ref.at[j * hx:(j + 1) * hx]))
    pos = pos_ref[...]
    bu_t, bv_t = bu_ref[...].T, bv_ref[...].T
    scale = 1.0 / math.sqrt(hd)
    selfs, qvs = [], []
    for h in range(n_heads):
        q = qin[h // hx, 0, h % hx].astype(F32)
        qu = (q + bu_t[:, h:h + 1]).astype(BF16).astype(F32)
        qvs.append((q + bv_t[:, h:h + 1]).astype(BF16))
        selfs.append(jnp.sum(qu * qin[h // hx, 1, h % hx].astype(F32), axis=0, keepdims=True))
        for j in range(n_slots):
            s_ref[j, h:h + 1, :] = jnp.sum(kc[h, j].astype(F32) * qu, axis=0, keepdims=True)
    self_score = jnp.concatenate(selfs, axis=0)
    rel_all = dot(rel_diag[...], jnp.concatenate(qvs, axis=0), NN)
    rel_all = [rel_all[r * n_heads:(r + 1) * n_heads] for r in range(n_slots)][::-1]
    shift = n_slots - 1 - pos
    bit = 1
    while bit < n_slots:
        take = (shift // bit) % 2 == 1
        rel_all = [jnp.where(take, rel_all[j + bit], rel_all[j]) if j + bit < n_slots else rel_all[j] for j in range(n_slots)]
        bit *= 2
    sc = []
    for j in range(n_slots):
        content = jnp.where(pos == j, self_score, s_ref[j])
        sc.append(jnp.where(pos >= j, (content + rel_all[j]) * scale, -1e30))
    top = functools.reduce(jnp.maximum, sc)
    ex = [jnp.exp(v - top) for v in sc]
    tot = functools.reduce(jnp.add, ex)
    probs = [(v / tot).astype(BF16).astype(F32) for v in ex]
    self_prob = functools.reduce(jnp.add, [jnp.where(pos == j, probs[j], 0.0) for j in range(n_slots)])
    for j in range(n_slots):
        p_ref[j] = jnp.where(pos == j, 0.0, probs[j])
    p_ref[n_slots] = self_prob
    c_v.wait()
    for h in range(n_heads):
        acc = p_ref[n_slots, h:h + 1, :] * qin[h // hx, 2, h % hx].astype(F32)
        for j in range(n_slots):
            acc = acc + p_ref[j, h:h + 1, :] * vc[h, j].astype(F32)
        o_t[h * hd:(h + 1) * hd, :] = acc
    oall[x] = o_t[...].T.astype(BF16)
    half = rows // 2

    def o_unit(xx, h):
        return oall.at[xx, h * half:(h + 1) * half]

    x_start("o", o_unit)
    up_relay(1)
    c_wo.wait()
    arrived(wo_land.at[1 - c], "wo")
    wo[...] = jnp.concatenate([wo_land[0], wo_land[1]], axis=1)

    def out_proj(px):
        g = xof[px]
        part = dot(oall[g], wo[...], NN).astype(BF16)
        st1[g] = part.reshape(ny, qr, dx)
        for i, key in ((2, "O"), (1, "D"), (ny - 1, "U")):
            send(st1.at[g, yp(i)], in1.at[y, g], dev(x, c, yp(i)), ("r1y", px, key))
        in1[y, g] = st1[g, y]

    x_relay("o", o_unit, "L")
    x_relay("o", o_unit, "R")
    up_send(2)
    out_proj("S")
    x_wait("o", o_unit, "L", 1)
    out_proj("L")
    x_wait("o", o_unit, "R", 0)
    out_proj("R")
    x_wait("o", o_unit, "O", 0)
    x_wait("o", o_unit, "O", 1)
    out_proj("O")
    gain_m = jnp.concatenate([gall[2 * x, 1:2, :], gall[2 * x + 1, 1:2, :]], axis=1)
    for px in "SLRO":
        for key in "DUO":
            arrived(in1.at[yof[key], xof[px]], ("r1y", px, key))
    for g in range(nx):
        acc = in1[0, g].astype(F32)
        for k in range(1, ny):
            acc = acc + in1[k, g].astype(F32)
        hbuf[g * qr:(g + 1) * qr, :] = xall[g, rowsl(y * qr, qr), lanes(dx, x)].astype(F32) + acc
    h = hbuf[...]
    sq = jnp.sum(h * h, axis=1, keepdims=True)
    sq = jnp.broadcast_to(sq, (rows, rows)).T[:8]
    st_s[...] = sq
    st_r[x] = sq
    for i, key in ((2, "O"), (1, "L"), (nx - 1, "R")):
        send(st_s, st_r.at[x], dev(xp(i), c, y), ("st", key))
    up_send(3)
    for key in "LRO":
        arrived(st_r.at[xof[key]], ("st", key))
    tot = st_r[0]
    for j in range(1, nx):
        tot = tot + st_r[j]
    rstd = lax.rsqrt(tot * (1.0 / d_model) + NORM_EPS)
    rstd = jnp.broadcast_to(rstd[0:1], (rows, rows)).T[:, 0:1]
    mall[y, :, lanes(dx, x)] = (hbuf[...] * rstd * gain_m).astype(BF16)

    def m_unit(xx, yy, h):
        return mall.at[yy, h * half:(h + 1) * half, lanes(dx, xx)]

    def m_x(xx, h):
        return m_unit(xx, y, h)

    x_start("mx", m_x)
    y_send("my", m_unit, "S", 0)
    y_send("my", m_unit, "S", 1)
    x_relay("mx", m_x, "L")
    y_send("my", m_unit, "L", 0)
    x_relay("mx", m_x, "R")
    y_send("my", m_unit, "R", 1)
    up_relay(2)
    for frm, h in (("L", 1), ("R", 0), ("O", 0), ("O", 1)):
        x_wait("mx", m_x, frm, h)
        y_send("my", m_unit, frm, h)
    up_relay(3)
    c_up.wait()
    arrived(wup.at[2 * x + 1 - c], "uown")
    for p in range(4):
        for key in "LRO":
            arrived(wup.at[2 * xof[key] + 1 - c, UP_PARTS[p]:UP_PARTS[p + 1]], ("us", p, key))

    def z_unit(py):
        return lambda xx, h: zall.at[yof[py], h * half:(h + 1) * half, lanes(fx, xx)]

    def hidden(py):
        z = dot(mall[yof[py]], wup[...].reshape(d_model, fx), NN)
        zall[yof[py], :, lanes(fx, x)] = jax.nn.gelu(z, approximate=True).astype(BF16)
        x_start(("z", py), z_unit(py))

    def z_relay(py):
        x_relay(("z", py), z_unit(py), "L")
        x_relay(("z", py), z_unit(py), "R")

    def down(py):
        for frm, h in (("L", 1), ("R", 0), ("O", 0), ("O", 1)):
            x_wait(("z", py), z_unit(py), frm, h)
        part = dot(zall[yof[py]], wdn[...].reshape(dx, ff), NT).astype(BF16)
        if py == "S":
            in2[y] = part
        else:
            k = "DUO".index(py)
            st2[k] = part
            send(st2.at[k], in2.at[y], dev(x, c, yof[py]), ("r2y", {"D": "U", "U": "D", "O": "O"}[py]))

    hidden("S")
    z_relay("S")
    for px in "SLRO":
        y_relay("my", m_unit, px, "D")
        y_relay("my", m_unit, px, "U")
    for px in "SLRO":
        y_wait("my", m_unit, px, "D", 1)
    hidden("D")
    for px in "SLRO":
        y_wait("my", m_unit, px, "U", 0)
    hidden("U")
    c_dn.wait()
    arrived(wdn.at[1 - c], "dn")
    z_relay("D")
    down("S")
    z_relay("U")
    for px in "SLRO":
        y_wait("my", m_unit, px, "O", 0)
        y_wait("my", m_unit, px, "O", 1)
    hidden("O")
    down("D")
    z_relay("O")
    down("U")
    down("O")
    for key in "DUO":
        arrived(in2.at[yof[key]], ("r2y", key))
    acc = in2[0].astype(F32)
    for k in range(1, ny):
        acc = acc + in2[k].astype(F32)
    yst[...] = (hbuf[...] + acc).astype(BF16).reshape(nx, qr, dx)
    for i, key in ((2, "O"), (1, "L"), (nx - 1, "R")):
        send(yst.at[xp(i)], yfull.at[y, :, lanes(dx, x)], dev(xp(i), c, y), ("yx", key))
    yfull[y, :, lanes(dx, x)] = yst[x]
    for px in "SLRO":
        blk = yfull.at[y, :, lanes(dx, xof[px])]
        if px != "S":
            arrived(blk, ("yx", px))
        for i, key in ((1, "D"), (ny - 1, "U"), (2, "O")):
            send(blk, blk, dev(x, c, yp(i)), ("yy", px, key))
    for px in "SLRO":
        for key in "DUO":
            arrived(yfull.at[yof[key], :, lanes(dx, xof[px])], ("yy", px, key))
    outs.append(local(yfull, y_ref))
    for cp in pending:
        cp.wait_send()
    for cp in outs:
        cp.wait()
    assert len(ids) <= N_REMOTE and n_local[0] <= N_LOCAL


def solution(mesh):
    nx, ny = mesh.shape["wg"] // 2, mesh.shape["tp"]
    tok_axes = ("dp", "wg")
    in_specs = (P(tok_axes, None), P("wg"), P("wg"), P("wg", None, "tp", None), P("wg", "tp", None), P("tp", None, "wg"), P("wg", "tp"), P("tp", "wg"), P("tp", None), P("tp", None), P(None, None), P(tok_axes, "tp", None, None), P(tok_axes, "tp", None, None), P(tok_axes))
    out_specs = (P(tok_axes, None), P(tok_axes, "tp", None), P(tok_axes, "tp", None))

    def device_step(tokens, gain_attn, gain_mlp, w_qkv, w_rel, w_out, w_up, w_down, bias_u, bias_v, rel_table, k_cache, v_cache, positions):
        rows, d_model = tokens.shape
        ds = gain_attn.shape[0]
        dx = 2 * ds
        _, n_heads, n_slots, hd = k_cache.shape
        hx = n_heads // nx
        hw = n_heads * hd
        ff = w_up.shape[1]
        fx = ff // nx
        qr = rows // ny
        any_spec = pl.BlockSpec(memory_space=pl.ANY)
        vmem_spec = pl.BlockSpec(memory_space=pltpu.VMEM)
        vm = pltpu.VMEM
        scratch = [
            vm((nx, rows, d_model), BF16),
            vm((nx, rows, d_model), BF16),
            vm((2, ds), F32),
            vm((2 * nx, 2, ds), F32),
            vm((1, d_model), F32),
            vm((2, 3, nx, hd, ds), BF16),
            vm((3, nx, hd, dx), BF16),
            vm((3, hx, hd, d_model), BF16),
            vm((nx - 1, 3, hx, hd, rows), BF16),
            vm((nx, 3, hx, hd, rows), BF16),
            vm((n_heads, n_slots, hd, rows), BF16),
            vm((n_heads, n_slots, hd, rows), BF16),
            vm((hw, ds), BF16),
            vm((2, n_slots // 2, hw), F32),
            vm((n_slots // 2, hw), F32),
            vm((nx, n_slots // 2, hw), F32),
            vm((2, n_slots // 2, hw), F32),
            vm((n_slots * n_heads, hw), BF16),
            vm((n_slots, n_heads, rows), F32),
            vm((n_slots + 1, n_heads, rows), F32),
            vm((hw, rows), F32),
            vm((nx, rows, hw), BF16),
            vm((2, hw, ds), BF16),
            vm((hw, dx), BF16),
            vm((nx, ny, qr, dx), BF16),
            vm((ny, nx, qr, dx), BF16),
            vm((rows, dx), F32),
            vm((8, rows), F32),
            vm((nx, 8, rows), F32),
            vm((ny, rows, d_model), BF16),
            vm((2 * nx, ds, fx), BF16),
            vm((ny, rows, ff), BF16),
            vm((2, ds, ff), BF16),
            vm((ny - 1, rows, dx), BF16),
            vm((ny, rows, dx), BF16),
            vm((nx, qr, dx), BF16),
            vm((ny, qr, d_model), BF16),
            pltpu.SemaphoreType.DMA((N_REMOTE,)),
            pltpu.SemaphoreType.DMA((N_REMOTE,)),
            pltpu.SemaphoreType.DMA((N_LOCAL,)),
        ]
        y, kn, vn = pl.pallas_call(
            functools.partial(layer_kernel, nx, ny),
            out_shape=(
                jax.ShapeDtypeStruct((ny, qr, d_model), BF16),
                jax.ShapeDtypeStruct((n_heads, hd, rows), BF16),
                jax.ShapeDtypeStruct((n_heads, hd, rows), BF16),
            ),
            in_specs=[any_spec, vmem_spec, vmem_spec, any_spec, any_spec, any_spec, any_spec, any_spec, vmem_spec, vmem_spec, vmem_spec, any_spec, any_spec, vmem_spec],
            out_specs=(any_spec, any_spec, any_spec),
            scratch_shapes=scratch,
            compiler_params=pltpu.CompilerParams(collective_id=0, has_side_effects=True, vmem_limit_bytes=60 * 2**20),
        )(
            tokens, gain_attn, gain_mlp, w_qkv.transpose(1, 2, 3, 0).reshape(3, nx, hx, hd, ds), w_rel.transpose(1, 2, 0).reshape(hw, ds), w_out.reshape(hw, ds),
            w_up, w_down.T, bias_u, bias_v, rel_table, k_cache.transpose(1, 2, 3, 0), v_cache.transpose(1, 2, 3, 0), positions[None, :],
        )
        return y.reshape(rows, d_model), kn.transpose(2, 0, 1), vn.transpose(2, 0, 1)

    return jax.shard_map(device_step, mesh=mesh, in_specs=in_specs, out_specs=out_specs, check_vma=False)
```

time: 146 us -> 124 us (0.85)
  Pallas kernels: 138 us -> 119 us
  local copies, waits for them, and re-layouts: 6.76 us -> 4.27 us
    pallas_call x1, Pallas kernels: 138 us -> 119 us  [device_step(): pl.pallas_call(functools.partial(layer_kernel, nx, ny), out_shape=(jax.Sh...]
    broadcast_in_dim x2 -> x0, local copies, waits for them, and re-layouts: 2.49 us -> none  [the longest x1 1.25 us: device_step(): gain_attn[None, :]]
where the time goes in v2:
time: 124 us
  Pallas kernels  119 us (96%)
  local copies, waits for them, and re-layouts  4.27 us (3%)
    pallas_call x1, Pallas kernels, device_step(): pl.pallas_call(functools.partial(layer_kernel, nx, ny), out_shape=(jax.Sh...  119 us
    unnamed x5, local copies, waits for them, and re-layouts  4.27 us

profile of v2, /device:TPU:96, one launch (start us, length us, event | category | flops | bytes accessed | tf_op | source)
XLA Modules:
  0.0 124.0 jit_solution(9179162199225580898)
XLA Ops:
  0.6 119.1 %shard_map.157 = (bf16[4,32,2560]{2,1,0:T(8,128)(2,1)}, bf16[8,80,128]{2,1,0:T(8,128)(2,1)}, bf16[8,80,128]{2,1,0:T(8,128)(2,1)}) custom-call(bf16[128,2560]{1,0:T(8,128)(2,1)} %tok_ref.1, f32[320]{0:T(512)} %ga_ref.1, f32[320]{0:T(512)} %gm_ref.1, bf16[3,4,2,80,320]{4,3,2,1,0:T(8,128)(2,1)} %bitcast.17, bf16[640,320]{1,0:T(8,128)(2,1)} %bitcast.19, ...), custom_call_target="tpu_custom_call" | custom-call | tf_op jit(solution)/shard_map/pallas_call | solution.py:507
  119.8 0.0 copy-start
  119.8 2.0 %copy.20 = bf16[128,2560]{1,0:T(8,128)(2,1)} copy(bf16[128,2560]{1,0:T(8,128)(2,1)} %bitcast.18) | data formatting | bytes 1310720
  121.8 1.6 %copy.21 = bf16[128,8,80]{0,2,1:T(8,128)(2,1)} copy(bf16[128,8,80]{0,2,1:T(8,128)(2,1)} %bitcast.22) | data formatting | bytes 327680
  123.4 0.0 copy-done
  123.4 0.7 copy.22
Async XLA Ops:
  119.8 3.6 %copy-start = (bf16[8,80,128]{2,1,0:T(8,128)(2,1)S(1)}, bf16[8,80,128]{2,1,0:T(8,128)(2,1)}, u32[]{:S(2)}) copy-start(bf16[8,80,128]{2,1,0:T(8,128)(2,1)} %get-tuple-element.8) | copy-start | bytes 491524

commit v3 on v2

--- a/solution.py
+++ b/solution.py
@@ -14,9 +14,9 @@
 F32 = jnp.float32
 NT = (((1,), (1,)), ((), ()))
 NN = (((1,), (0,)), ((), ()))
-N_REMOTE = 224
+N_REMOTE = 256
 N_LOCAL = 32
-UP_PARTS = (0, 96, 128, 272, 320)
+UP_PARTS = (0, 64, 128, 272, 320)
 
 
 def dot(a, b, dims):
@@ -25,7 +25,7 @@
 
 def layer_kernel(nx, ny, tok_ref, ga_ref, gm_ref, wqkv_ref, wrel_ref, wout_ref, wup_ref, wdn_ref, bu_ref, bv_ref, relt_ref, kc_ref, vc_ref, pos_ref,
                  y_ref, kn_ref, vn_ref,
-                 xall, nall, gst, gall, gain, wq_land, wpk, wq, qst, qin, kc, vc, wrel, rsend, rsib, rland, rfull, rel_diag, s_ref, p_ref, o_t, oall, wo_land, wo,
+                 xall, nall, qacc, gst, gall, gain, wq_land, wpk, wq, qst, qin, kc, vc, wrel, rsend, rsib, rland, rfull, rel_diag, s_ref, p_ref, o_t, oall, wo_land, wo,
                  st1, in1, hbuf, st_s, st_r, mall, wup, zall, wdn, st2, in2, yst, yfull,
                  ss, rs, ls):
     w = lax.axis_index("wg")
@@ -83,10 +83,9 @@
     def rowsl(start, size):
         return pl.ds(pl.multiple_of(start, 16), size)
 
-    def x_start(name, unit, own=None):
-        own = own or (lambda h: unit(x, h))
+    def x_start(name, unit):
         for h, to, frm in ((0, right, "L"), (1, left, "R"), (1, right, "L"), (0, left, "R")):
-            send(own(h), unit(x, h), to, (name, frm, h))
+            send(unit(x, h), unit(x, h), to, (name, frm, h))
 
     def x_relay(name, unit, frm):
         h, to = (0, right) if frm == "L" else (1, left)
@@ -136,7 +135,8 @@
     def tok_x(xx, h):
         return tok_unit(xx, y, h)
 
-    x_start("tx", tok_x, lambda h: tok_ref.at[rowsl(y * qr + h * hq, hq)])
+    c_x.wait()
+    x_start("tx", tok_x)
     send(wqkv_ref.at[:, :, 1 - c], wq_land.at[c], sib, "wqs")
     send(gst, gall.at[w], sib, ("g", 0))
     for i in range(1, nx):
@@ -156,11 +156,15 @@
     arrived(wq_land.at[1 - c], "wqs")
     for s in range(3):
         for j in range(nx):
-            wpk[s, j] = jnp.concatenate([wq_land[0, s, j], wq_land[1, s, j]], axis=1)
+            wpk[j, s * hd:(s + 1) * hd, :] = jnp.concatenate([wq_land[0, s, j], wq_land[1, s, j]], axis=1)
+
+    def wq_unit(cc, xx):
+        return wq.at[rowsl(cc * (3 * hd), 3 * hd), lanes(dx, xx)]
+
     for i, key in ((1, "L"), (nx - 1, "R"), (2, "O")):
-        send(wpk.at[:, xp(i)], wq.at[:, c, :, lanes(dx, x)], dev(xp(i), c, y), ("wx", key))
-    wq[:, c, :, lanes(dx, x)] = wpk[:, x]
-    send(wpk.at[:, x], wq.at[:, c, :, lanes(dx, x)], sib, ("ws", "S"))
+        send(wpk.at[xp(i)], wq_unit(c, x), dev(xp(i), c, y), ("wx", key))
+    wq[rowsl(c * (3 * hd), 3 * hd), lanes(dx, x)] = wpk[x]
+    send(wpk.at[x], wq_unit(c, x), sib, ("ws", "S"))
     arrived(rsib, "r0")
     rland[x] = rsend[c] + rsib[...]
     for i, key in ((1, "L"), (nx - 1, "R"), (2, "O")):
@@ -193,41 +197,56 @@
     for i in range(1, nx):
         arrived(gall.at[2 * lax.rem(x + nx - i, nx) + 1 - c], ("gs", i))
     gain[...] = jnp.concatenate([gall[j, 0:1, :] for j in range(2 * nx)], axis=1)
-    blk_rows = 32
-
-    def norm_group(g):
-        def norm_block(r, carry):
-            b = pl.ds(pl.multiple_of(r * blk_rows, blk_rows), blk_rows)
-            v = xall[g, b, :].astype(F32)
-            ms = jnp.mean(v * v, axis=-1, keepdims=True)
-            nall[g, b, :] = (v * lax.rsqrt(ms + NORM_EPS) * gain[...]).astype(BF16)
-            return carry
-
-        lax.fori_loop(0, rows // blk_rows, norm_block, 0)
-
-    c_x.wait()
-    norm_group(x)
+    def norm_block(px, yy):
+        v = xall[xof[px], rowsl(yy * qr, qr), :].astype(F32)
+        ms = jnp.mean(v * v, axis=-1, keepdims=True)
+        nall[rowsl("ORLS".index(px) * rows + yy * qr, qr), :] = (v * lax.rsqrt(ms + NORM_EPS) * gain[...]).astype(BF16)
+
+    def norm_own(r, carry):
+        norm_block("S", r)
+        return carry
+
+    lax.fori_loop(0, ny, norm_own, 0)
+    for px in "LRO":
+        norm_block(px, y)
     for px, frm in (("L", "D"), ("R", "U"), ("L", "U"), ("R", "D"), ("O", "D"), ("O", "U")):
         y_relay("ty", tok_unit, px, frm)
-    for key in "LRO":
-        blk = wq.at[:, c, :, lanes(dx, xof[key])]
-        arrived(blk, ("wx", key))
-        send(blk, blk, sib, ("ws", key))
     for px in "LRO":
-        for frm, h in (("D", 1), ("U", 0), ("O", 0), ("O", 1)):
-            y_wait("ty", tok_unit, px, frm, h)
-        norm_group(xof[px])
-    for key in "SLRO":
-        arrived(wq.at[:, 1 - c, :, lanes(dx, xof[key])], ("ws", key))
-    wqv = wq[...].reshape(3 * hx * hd, d_model)
-    for i, key in ((2, "O"), (1, "L"), (nx - 1, "R"), (0, "S")):
-        g = xp(i)
-        res = dot(wqv, nall[g], NT).astype(BF16).reshape(3, hx, hd, rows)
-        if i:
-            qst[i - 1] = res
-            send(qst.at[i - 1], qin.at[x], dev(g, c, y), ("q", key))
-        else:
-            qin[x] = res
+        y_wait("ty", tok_unit, px, "D", 1)
+        norm_block(px, yof["D"])
+        y_wait("ty", tok_unit, px, "U", 0)
+        norm_block(px, yof["U"])
+    def qkv_part(key, p):
+        k = lanes(dx, xof[key])
+        return dot(wq[:, k], nall[2 * p * rows:2 * (p + 1) * rows, k], NT)
+
+    def wq_relay(key):
+        arrived(wq_unit(c, xof[key]), ("wx", key))
+        send(wq_unit(c, xof[key]), wq_unit(c, xof[key]), sib, ("ws", key))
+
+    wq_relay("L")
+    wq_relay("R")
+    for px in "LRO":
+        y_wait("ty", tok_unit, px, "O", 0)
+        y_wait("ty", tok_unit, px, "O", 1)
+        norm_block(px, yof["O"])
+    wq_relay("O")
+    arrived(wq_unit(1 - c, x), ("ws", "S"))
+    for p in range(2):
+        qacc[p] = qkv_part("S", p)
+    for key in "LR":
+        arrived(wq_unit(1 - c, xof[key]), ("ws", key))
+    for p in range(2):
+        qacc[p] += qkv_part("L", p) + qkv_part("R", p)
+    arrived(wq_unit(1 - c, xof["O"]), ("ws", "O"))
+    for p, pair in enumerate((((2, "O"), (1, "L")), ((nx - 1, "R"), (0, "S")))):
+        res = (qacc[p] + qkv_part("O", p)).astype(BF16).reshape(hx, 3, hd, 2 * rows)
+        for k, (i, key) in enumerate(pair):
+            if i:
+                qst[i - 1] = res[:, :, :, k * rows:(k + 1) * rows]
+                send(qst.at[i - 1], qin.at[x], dev(xp(i), c, y), ("q", key))
+            else:
+                qin[x] = res[:, :, :, k * rows:(k + 1) * rows]
     up_send(1)
     for key in "LRO":
         arrived(rland.at[xof[key]], ("r1", key))
@@ -249,17 +268,17 @@
         arrived(qin.at[xof[key]], ("q", key))
     outs = []
     for j in range(nx):
-        outs.append(local(qin.at[j, 1], kn_ref.at[j * hx:(j + 1) * hx]))
-        outs.append(local(qin.at[j, 2], vn_ref.at[j * hx:(j + 1) * hx]))
+        outs.append(local(qin.at[j, :, 1], kn_ref.at[j * hx:(j + 1) * hx]))
+        outs.append(local(qin.at[j, :, 2], vn_ref.at[j * hx:(j + 1) * hx]))
     pos = pos_ref[...]
     bu_t, bv_t = bu_ref[...].T, bv_ref[...].T
     scale = 1.0 / math.sqrt(hd)
     selfs, qvs = [], []
     for h in range(n_heads):
-        q = qin[h // hx, 0, h % hx].astype(F32)
+        q = qin[h // hx, h % hx, 0].astype(F32)
         qu = (q + bu_t[:, h:h + 1]).astype(BF16).astype(F32)
         qvs.append((q + bv_t[:, h:h + 1]).astype(BF16))
-        selfs.append(jnp.sum(qu * qin[h // hx, 1, h % hx].astype(F32), axis=0, keepdims=True))
+        selfs.append(jnp.sum(qu * qin[h // hx, h % hx, 1].astype(F32), axis=0, keepdims=True))
         for j in range(n_slots):
             s_ref[j, h:h + 1, :] = jnp.sum(kc[h, j].astype(F32) * qu, axis=0, keepdims=True)
     self_score = jnp.concatenate(selfs, axis=0)
@@ -285,7 +304,7 @@
     p_ref[n_slots] = self_prob
     c_v.wait()
     for h in range(n_heads):
-        acc = p_ref[n_slots, h:h + 1, :] * qin[h // hx, 2, h % hx].astype(F32)
+        acc = p_ref[n_slots, h:h + 1, :] * qin[h // hx, h % hx, 2].astype(F32)
         for j in range(n_slots):
             acc = acc + p_ref[j, h:h + 1, :] * vc[h, j].astype(F32)
         o_t[h * hd:(h + 1) * hd, :] = acc
@@ -309,10 +328,10 @@
             send(st1.at[g, yp(i)], in1.at[y, g], dev(x, c, yp(i)), ("r1y", px, key))
         in1[y, g] = st1[g, y]
 
+    out_proj("S")
     x_relay("o", o_unit, "L")
     x_relay("o", o_unit, "R")
     up_send(2)
-    out_proj("S")
     x_wait("o", o_unit, "L", 1)
     out_proj("L")
     x_wait("o", o_unit, "R", 0)
@@ -328,7 +347,9 @@
         acc = in1[0, g].astype(F32)
         for k in range(1, ny):
             acc = acc + in1[k, g].astype(F32)
-        hbuf[g * qr:(g + 1) * qr, :] = xall[g, rowsl(y * qr, qr), lanes(dx, x)].astype(F32) + acc
+        acc = xall[g, rowsl(y * qr, qr), lanes(dx, x)].astype(F32) + acc
+        for k in range(2):
+            hbuf[k * half + g * hq:k * half + (g + 1) * hq, :] = acc[k * hq:(k + 1) * hq]
     h = hbuf[...]
     sq = jnp.sum(h * h, axis=1, keepdims=True)
     sq = jnp.broadcast_to(sq, (rows, rows)).T[:8]
@@ -346,101 +367,198 @@
     rstd = jnp.broadcast_to(rstd[0:1], (rows, rows)).T[:, 0:1]
     mall[y, :, lanes(dx, x)] = (hbuf[...] * rstd * gain_m).astype(BF16)
 
-    def m_unit(xx, yy, h):
-        return mall.at[yy, h * half:(h + 1) * half, lanes(dx, xx)]
-
-    def m_x(xx, h):
-        return m_unit(xx, y, h)
-
-    x_start("mx", m_x)
-    y_send("my", m_unit, "S", 0)
-    y_send("my", m_unit, "S", 1)
-    x_relay("mx", m_x, "L")
-    y_send("my", m_unit, "L", 0)
-    x_relay("mx", m_x, "R")
-    y_send("my", m_unit, "R", 1)
+    sub = half // 2
+
+    def piece(h, k=None):
+        return slice(h * half, (h + 1) * half) if k is None else slice(h * half + k * sub, h * half + (k + 1) * sub)
+
+    def m_unit(px, py, h, k=None):
+        return mall.at[yof[py], piece(h, k), lanes(dx, xof[px])]
+
+    def z_unit(px, py, h, k=None):
+        return zall.at[yof[py], piece(h, k), lanes(fx, xof[px])]
+
+    def xs_send(name, unit, py, h):
+        blk = unit("S", py, h)
+        send(blk, blk, right, (name, py, h, "L"))
+        send(blk, blk, left, (name, py, h, "R"))
+
+    direct = set()
+
+    def xs_direct(name, unit, py, h):
+        direct.add((name, py, h))
+        blk = unit("S", py, h)
+        send(blk, blk, dev(xp(2), c, y), (name, py, h, "O"))
+        xs_send(name, unit, py, h)
+
+    def xs_near(name, unit, py, h):
+        for frm in "LR":
+            arrived(unit(frm, py, h), (name, py, h, frm))
+
+    def xs_relay(name, unit, py, h):
+        for frm, to, k in (("L", right, 0), ("R", left, 1)):
+            arrived(unit(frm, py, h), (name, py, h, frm))
+            blk = unit(frm, py, h, k)
+            send(blk, blk, to, (name, py, h, "O", k))
+
+    def xs_last(name, unit, py, h):
+        if (name, py, h) in direct:
+            arrived(unit("O", py, h), (name, py, h, "O"))
+            return
+        for k in range(2):
+            arrived(unit("O", py, h, k), (name, py, h, "O", k))
+
+    def ys_send(px, h):
+        blk = m_unit(px, "S", h)
+        send(blk, blk, above, ("my", px, h, "D"))
+        send(blk, blk, below, ("my", px, h, "U"))
+
+    def ys_relay(px, h):
+        for frm, to, k in (("D", above, 0), ("U", below, 1)):
+            arrived(m_unit(px, frm, h), ("my", px, h, frm))
+            blk = m_unit(px, frm, h, k)
+            send(blk, blk, to, ("my", px, h, "O", k))
+
+    def ys_last(h):
+        for px in "SLRO":
+            for k in range(2):
+                arrived(m_unit(px, "O", h, k), ("my", px, h, "O", k))
+
+    def hidden(blocks, spread=xs_send):
+        m = jnp.concatenate([mall[yof[py], piece(h), :] for py, h in blocks], axis=0)
+        z = dot(m, wup[...].reshape(d_model, fx), NN)
+        z = jax.nn.gelu(z, approximate=True).astype(BF16)
+        for k, (py, h) in enumerate(blocks):
+            zall[yof[py], piece(h), lanes(fx, x)] = z[k * half:(k + 1) * half]
+            spread("z", z_unit, py, h)
+
+    def down(blocks):
+        for py, h in blocks:
+            xs_last("z", z_unit, py, h)
+        z = jnp.concatenate([zall[yof[py], piece(h), :] for py, h in blocks], axis=0)
+        part = dot(z, wdn[...].reshape(dx, ff), NT).astype(BF16)
+        for k, (py, h) in enumerate(blocks):
+            blk = part[k * half:(k + 1) * half]
+            if py == "S":
+                in2[y, h] = blk
+            else:
+                j = "DUO".index(py)
+                st2[j, h] = blk
+                send(st2.at[j, h], in2.at[y, h], dev(x, c, yof[py]), ("r2y", {"D": "U", "U": "D", "O": "O"}[py], h))
+
+    def y_unit(px, py, h):
+        return yfull.at[yof[py], h * hq:(h + 1) * hq, lanes(dx, xof[px])]
+
+    def yy_send(px, h):
+        blk = y_unit(px, "S", h)
+        for i, key in ((2, "O"), (1, "D"), (ny - 1, "U")):
+            send(blk, blk, dev(x, c, yp(i)), ("yy", px, h, key))
+
+    def finish(h):
+        for key in "DUO":
+            arrived(in2.at[yof[key], h], ("r2y", key, h))
+        acc = in2[0, h].astype(F32)
+        for k in range(1, ny):
+            acc = acc + in2[k, h].astype(F32)
+        yst[h] = (hbuf[piece(h), :] + acc).astype(BF16).reshape(nx, hq, dx)
+        for i, key in ((2, "O"), (1, "L"), (nx - 1, "R")):
+            send(yst.at[h, xp(i)], y_unit("S", "S", h), dev(xp(i), c, y), ("yx", key, h))
+        yfull[y, h * hq:(h + 1) * hq, lanes(dx, x)] = yst[h, x]
+        yy_send("S", h)
+
+    def y_forward(h):
+        for px in "LRO":
+            arrived(y_unit(px, "S", h), ("yx", px, h))
+            yy_send(px, h)
+
+    xs_direct("mx", m_unit, "S", 0)
+    ys_send("S", 0)
+    xs_direct("mx", m_unit, "S", 1)
+    ys_send("S", 1)
     up_relay(2)
-    for frm, h in (("L", 1), ("R", 0), ("O", 0), ("O", 1)):
-        x_wait("mx", m_x, frm, h)
-        y_send("my", m_unit, frm, h)
     up_relay(3)
+    xs_last("mx", m_unit, "S", 0)
+    ys_send("O", 0)
+    xs_near("mx", m_unit, "S", 0)
+    ys_send("L", 0)
+    ys_send("R", 0)
     c_up.wait()
     arrived(wup.at[2 * x + 1 - c], "uown")
     for p in range(4):
         for key in "LRO":
             arrived(wup.at[2 * xof[key] + 1 - c, UP_PARTS[p]:UP_PARTS[p + 1]], ("us", p, key))
-
-    def z_unit(py):
-        return lambda xx, h: zall.at[yof[py], h * half:(h + 1) * half, lanes(fx, xx)]
-
-    def hidden(py):
-        z = dot(mall[yof[py]], wup[...].reshape(d_model, fx), NN)
-        zall[yof[py], :, lanes(fx, x)] = jax.nn.gelu(z, approximate=True).astype(BF16)
-        x_start(("z", py), z_unit(py))
-
-    def z_relay(py):
-        x_relay(("z", py), z_unit(py), "L")
-        x_relay(("z", py), z_unit(py), "R")
-
-    def down(py):
-        for frm, h in (("L", 1), ("R", 0), ("O", 0), ("O", 1)):
-            x_wait(("z", py), z_unit(py), frm, h)
-        part = dot(zall[yof[py]], wdn[...].reshape(dx, ff), NT).astype(BF16)
-        if py == "S":
-            in2[y] = part
-        else:
-            k = "DUO".index(py)
-            st2[k] = part
-            send(st2.at[k], in2.at[y], dev(x, c, yof[py]), ("r2y", {"D": "U", "U": "D", "O": "O"}[py]))
-
-    hidden("S")
-    z_relay("S")
+    hidden([("S", 0)], xs_direct)
+    xs_last("mx", m_unit, "S", 1)
+    ys_send("O", 1)
+    xs_near("mx", m_unit, "S", 1)
+    ys_send("L", 1)
+    ys_send("R", 1)
+    hidden([("S", 1)], xs_direct)
+    for px in "SOLR":
+        ys_relay(px, 0)
+    hidden([("D", 0), ("U", 0)])
+    ys_last(0)
+    hidden([("O", 0)])
     for px in "SLRO":
-        y_relay("my", m_unit, px, "D")
-        y_relay("my", m_unit, px, "U")
-    for px in "SLRO":
-        y_wait("my", m_unit, px, "D", 1)
-    hidden("D")
-    for px in "SLRO":
-        y_wait("my", m_unit, px, "U", 0)
-    hidden("U")
+        ys_relay(px, 1)
+    xs_relay("z", z_unit, "D", 0)
+    xs_relay("z", z_unit, "U", 0)
+    hidden([("D", 1), ("U", 1)])
     c_dn.wait()
     arrived(wdn.at[1 - c], "dn")
-    z_relay("D")
-    down("S")
-    z_relay("U")
-    for px in "SLRO":
-        y_wait("my", m_unit, px, "O", 0)
-        y_wait("my", m_unit, px, "O", 1)
-    hidden("O")
-    down("D")
-    z_relay("O")
-    down("U")
-    down("O")
-    for key in "DUO":
-        arrived(in2.at[yof[key]], ("r2y", key))
-    acc = in2[0].astype(F32)
-    for k in range(1, ny):
-        acc = acc + in2[k].astype(F32)
-    yst[...] = (hbuf[...] + acc).astype(BF16).reshape(nx, qr, dx)
-    for i, key in ((2, "O"), (1, "L"), (nx - 1, "R")):
-        send(yst.at[xp(i)], yfull.at[y, :, lanes(dx, x)], dev(xp(i), c, y), ("yx", key))
-    yfull[y, :, lanes(dx, x)] = yst[x]
-    for px in "SLRO":
-        blk = yfull.at[y, :, lanes(dx, xof[px])]
-        if px != "S":
-            arrived(blk, ("yx", px))
-        for i, key in ((1, "D"), (ny - 1, "U"), (2, "O")):
-            send(blk, blk, dev(x, c, yp(i)), ("yy", px, key))
-    for px in "SLRO":
-        for key in "DUO":
-            arrived(yfull.at[yof[key], :, lanes(dx, xof[px])], ("yy", px, key))
+    xs_near("z", z_unit, "S", 0)
+    xs_near("z", z_unit, "S", 1)
+    down([("S", 0), ("S", 1)])
+    xs_relay("z", z_unit, "O", 0)
+    ys_last(1)
+    hidden([("O", 1)])
+    down([("D", 0), ("U", 0)])
+    xs_relay("z", z_unit, "D", 1)
+    xs_relay("z", z_unit, "U", 1)
+    down([("O", 0)])
+    xs_relay("z", z_unit, "O", 1)
+    down([("D", 1), ("U", 1)])
+    finish(0)
+    down([("O", 1)])
+    y_forward(0)
+    finish(1)
+    y_forward(1)
+    for h in range(2):
+        for px in "SLRO":
+            for key in "DUO":
+                arrived(y_unit(px, key, h), ("yy", px, h, key))
     outs.append(local(yfull, y_ref))
     for cp in pending:
         cp.wait_send()
     for cp in outs:
         cp.wait()
     assert len(ids) <= N_REMOTE and n_local[0] <= N_LOCAL
+
+
+def copy_kernel(*refs):
+    n = (len(refs) - 1) // 3
+    srcs, dsts, bufs, sems = refs[:n], refs[n:2 * n], refs[2 * n:3 * n], refs[3 * n]
+    ins = [pltpu.make_async_copy(srcs[i], bufs[i], sems.at[i]) for i in range(n)]
+    outs = [pltpu.make_async_copy(bufs[i], dsts[i], sems.at[n + i]) for i in range(n)]
+    for cp in ins:
+        cp.start()
+    for i in range(n):
+        ins[i].wait()
+        outs[i].start()
+    for cp in outs:
+        cp.wait()
+
+
+def copy_out(*arrays):
+    n = len(arrays)
+    any_spec = pl.BlockSpec(memory_space=pl.ANY)
+    return pl.pallas_call(
+        copy_kernel,
+        out_shape=tuple(jax.ShapeDtypeStruct(a.shape, a.dtype) for a in arrays),
+        in_specs=[any_spec] * n,
+        out_specs=tuple([any_spec] * n),
+        scratch_shapes=[pltpu.VMEM(a.shape, a.dtype) for a in arrays] + [pltpu.SemaphoreType.DMA((2 * n,))],
+    )(*arrays)
 
 
 def solution(mesh):
@@ -464,15 +582,16 @@
         vm = pltpu.VMEM
         scratch = [
             vm((nx, rows, d_model), BF16),
-            vm((nx, rows, d_model), BF16),
+            vm((nx * rows, d_model), BF16),
+            vm((2, 3 * hx * hd, 2 * rows), F32),
             vm((2, ds), F32),
             vm((2 * nx, 2, ds), F32),
             vm((1, d_model), F32),
             vm((2, 3, nx, hd, ds), BF16),
-            vm((3, nx, hd, dx), BF16),
-            vm((3, hx, hd, d_model), BF16),
-            vm((nx - 1, 3, hx, hd, rows), BF16),
-            vm((nx, 3, hx, hd, rows), BF16),
+            vm((nx, 3 * hd, dx), BF16),
+            vm((hx * 3 * hd, d_model), BF16),
+            vm((nx - 1, hx, 3, hd, rows), BF16),
+            vm((nx, hx, 3, hd, rows), BF16),
             vm((n_heads, n_slots, hd, rows), BF16),
             vm((n_heads, n_slots, hd, rows), BF16),
             vm((hw, ds), BF16),
@@ -496,9 +615,9 @@
             vm((2 * nx, ds, fx), BF16),
             vm((ny, rows, ff), BF16),
             vm((2, ds, ff), BF16),
-            vm((ny - 1, rows, dx), BF16),
-            vm((ny, rows, dx), BF16),
-            vm((nx, qr, dx), BF16),
+            vm((ny - 1, 2, rows // 2, dx), BF16),
+            vm((ny, 2, rows // 2, dx), BF16),
+            vm((2, nx, qr // 2, dx), BF16),
             vm((ny, qr, d_model), BF16),
             pltpu.SemaphoreType.DMA((N_REMOTE,)),
             pltpu.SemaphoreType.DMA((N_REMOTE,)),
@@ -519,6 +638,7 @@
             tokens, gain_attn, gain_mlp, w_qkv.transpose(1, 2, 3, 0).reshape(3, nx, hx, hd, ds), w_rel.transpose(1, 2, 0).reshape(hw, ds), w_out.reshape(hw, ds),
             w_up, w_down.T, bias_u, bias_v, rel_table, k_cache.transpose(1, 2, 3, 0), v_cache.transpose(1, 2, 3, 0), positions[None, :],
         )
-        return y.reshape(rows, d_model), kn.transpose(2, 0, 1), vn.transpose(2, 0, 1)
+        y, kn, vn = copy_out(y.reshape(rows, d_model), kn, vn)
+        return y, kn.transpose(2, 0, 1), vn.transpose(2, 0, 1)
 
     return jax.shard_map(device_step, mesh=mesh, in_specs=in_specs, out_specs=out_specs, check_vma=False)

time: 124 us -> 119 us (0.960)
  local copies, waits for them, and re-layouts: 4.27 us -> 0 us
    unnamed x5 -> x0, local copies, waits for them, and re-layouts: 4.27 us -> none
    pallas_call x1, Pallas kernels: 119 us -> 116 us  [device_step(): pl.pallas_call(functools.partial(layer_kernel, nx, ny), out_shape=(jax.Sh...]
    pallas_call x0 -> x1, Pallas kernels: none -> 2.08 us  [copy_out(): pl.pallas_call(copy_kernel, out_shape=tuple((jax.ShapeDtypeStruct(a.shape...]
where the time goes in v3:
time: 119 us; the launch traced here: 118 us
  Pallas kernels  118 us (99%)
    pallas_call x1, Pallas kernels, device_step(): pl.pallas_call(functools.partial(layer_kernel, nx, ny), out_shape=(jax.Sh...  116 us

profile of v3, /device:TPU:96, one launch (start us, length us, event | category | flops | bytes accessed | tf_op | source)
XLA Modules:
  0.0 118.4 jit_solution(17550471024229740505)
XLA Ops:
  0.6 115.5 %shard_map.157 = (bf16[4,32,2560]{2,1,0:T(8,128)(2,1)}, bf16[8,80,128]{2,1,0:T(8,128)(2,1)}, bf16[8,80,128]{2,1,0:T(8,128)(2,1)}) custom-call(bf16[128,2560]{1,0:T(8,128)(2,1)} %tok_ref.1, f32[320]{0:T(512)} %ga_ref.1, f32[320]{0:T(512)} %gm_ref.1, bf16[3,4,2,80,320]{4,3,2,1,0:T(8,128)(2,1)} %bitcast.17, bf16[640,320]{1,0:T(8,128)(2,1)} %bitcast.19, ...), custom_call_target="tpu_custom_call" | custom-call | tf_op jit(solution)/shard_map/pallas_call | solution.py:626
  116.2 2.1 %shard_map.158 = (bf16[128,2560]{1,0:T(8,128)(2,1)}, bf16[8,80,128]{2,1,0:T(8,128)(2,1)}, bf16[8,80,128]{2,1,0:T(8,128)(2,1)}) custom-call(bf16[128,2560]{1,0:T(8,128)(2,1)} %bitcast.18, bf16[8,80,128]{2,1,0:T(8,128)(2,1)} %get-tuple-element.10.refs_1_, bf16[8,80,128]{2,1,0:T(8,128)(2,1)} %get-tuple-element.11.refs_2_), custom_call_target="tpu_custom_call" | custom-call | tf_op jit(solution)/shard_map/pallas_call | solution.py:555

commit v4 on v3

--- a/solution.py
+++ b/solution.py
@@ -15,8 +15,8 @@
 NT = (((1,), (1,)), ((), ()))
 NN = (((1,), (0,)), ((), ()))
 N_REMOTE = 256
-N_LOCAL = 32
-UP_PARTS = (0, 64, 128, 272, 320)
+N_LOCAL = 40
+UP_PARTS = (0, 112, 160, 304, 320)
 
 
 def dot(a, b, dims):
@@ -25,7 +25,7 @@
 
 def layer_kernel(nx, ny, tok_ref, ga_ref, gm_ref, wqkv_ref, wrel_ref, wout_ref, wup_ref, wdn_ref, bu_ref, bv_ref, relt_ref, kc_ref, vc_ref, pos_ref,
                  y_ref, kn_ref, vn_ref,
-                 xall, nall, qacc, gst, gall, gain, wq_land, wpk, wq, qst, qin, kc, vc, wrel, rsend, rsib, rland, rfull, rel_diag, s_ref, p_ref, o_t, oall, wo_land, wo,
+                 xall, nall, qacc, ga, gm, relt, bu, bv, posv, gall, gain, wq_land, wpk, wq, qst, qin, kc, vc, wrel, rsend, rsib, rland, rfull, rel_diag, s_ref, p_ref, o_t, oall, wo_land, wo,
                  st1, in1, hbuf, st_s, st_r, mall, wup, zall, wdn, st2, in2, yst, yfull,
                  ss, rs, ls):
     w = lax.axis_index("wg")
@@ -109,22 +109,30 @@
     def y_wait(name, unit, px, frm, h):
         arrived(unit(xof[px], yof[frm], h), (name, px, frm, h))
 
+    barrier = pltpu.get_barrier_semaphore()
+    peers = [dev(xp(i), c, y) for i in range(1, nx)] + [dev(x, c, yp(i)) for i in range(1, ny)] + [sib]
+    for peer in peers:
+        pl.semaphore_signal(barrier, inc=1, device_id=peer, device_id_type=MESH)
+    c_small = [local(ga_ref, ga), local(gm_ref, gm)]
+    c_rel = [local(wrel_ref, wrel), local(relt_ref.at[:, lanes(dx, x)], relt)]
+    c_x = local(tok_ref, xall.at[x])
     c_wq = local(wqkv_ref.at[:, :, c], wq_land.at[c])
-    c_rel = local(wrel_ref, wrel)
-    c_x = local(tok_ref, xall.at[x])
+    c_bias = [local(bu_ref, bu), local(bv_ref, bv), local(pos_ref, posv)]
     c_k = local(kc_ref, kc)
     c_v = local(vc_ref, vc)
     c_wo = local(wout_ref, wo_land.at[c])
     c_up = local(wup_ref.at[:, lanes(fx, x)], wup.at[w])
     c_dn = local(wdn_ref, wdn.at[c])
-    gst[0:1, :] = ga_ref[...].reshape(1, ds)
-    gst[1:2, :] = gm_ref[...].reshape(1, ds)
-    gall[w] = gst[...]
-
-    barrier = pltpu.get_barrier_semaphore()
-    peers = [dev(xp(i), c, y) for i in range(1, nx)] + [dev(x, c, yp(i)) for i in range(1, ny)] + [sib]
-    for peer in peers:
-        pl.semaphore_signal(barrier, inc=1, device_id=peer, device_id_type=MESH)
+    for cp in c_rel:
+        cp.wait()
+    tab = jnp.where(c == 0, relt[:, :ds], relt[:, ds:])
+    hs = n_slots // 2
+    rsend[...] = dot(tab, wrel[...], NT).reshape(2, hs, hw)
+    for cp in c_small:
+        cp.wait()
+    gall[w, 0:1, :] = ga[...].reshape(1, ds)
+    gall[w, 1:2, :] = gm[...].reshape(1, ds)
+
     pl.semaphore_wait(barrier, len(peers))
 
     hq = qr // 2
@@ -138,15 +146,9 @@
     c_x.wait()
     x_start("tx", tok_x)
     send(wqkv_ref.at[:, :, 1 - c], wq_land.at[c], sib, "wqs")
-    send(gst, gall.at[w], sib, ("g", 0))
+    send(gall.at[w], gall.at[w], sib, ("g", 0))
     for i in range(1, nx):
-        send(gst, gall.at[w], dev(xp(i), c, y), ("g", i))
-    c_rel.wait()
-    tab = relt_ref[:, lanes(dx, x)]
-    tab = jnp.where(c == 0, tab[:, :ds], tab[:, ds:])
-    part = dot(tab, wrel[...], NT)
-    hs = n_slots // 2
-    rsend[...] = part.reshape(2, hs, hw)
+        send(gall.at[w], gall.at[w], dev(xp(i), c, y), ("g", i))
     send(rsend.at[1 - c], rsib, sib, "r0")
     x_relay("tx", tok_x, "L")
     y_send("ty", tok_unit, "L", 0)
@@ -226,11 +228,11 @@
 
     wq_relay("L")
     wq_relay("R")
+    wq_relay("O")
     for px in "LRO":
         y_wait("ty", tok_unit, px, "O", 0)
         y_wait("ty", tok_unit, px, "O", 1)
         norm_block(px, yof["O"])
-    wq_relay("O")
     arrived(wq_unit(1 - c, x), ("ws", "S"))
     for p in range(2):
         qacc[p] = qkv_part("S", p)
@@ -244,9 +246,11 @@
         for k, (i, key) in enumerate(pair):
             if i:
                 qst[i - 1] = res[:, :, :, k * rows:(k + 1) * rows]
-                send(qst.at[i - 1], qin.at[x], dev(xp(i), c, y), ("q", key))
+                send(qst.at[i - 1, :, 0:2], qin.at[x, :, 0:2], dev(xp(i), c, y), ("q", key))
             else:
                 qin[x] = res[:, :, :, k * rows:(k + 1) * rows]
+    for i, key in ((2, "O"), (1, "L"), (nx - 1, "R")):
+        send(qst.at[i - 1, :, 2], qin.at[x, :, 2], dev(xp(i), c, y), ("v", key))
     up_send(1)
     for key in "LRO":
         arrived(rland.at[xof[key]], ("r1", key))
@@ -265,13 +269,14 @@
     rel_diag[...] = jnp.where(keep, rel, 0.0).astype(BF16)
     c_k.wait()
     for key in "LRO":
-        arrived(qin.at[xof[key]], ("q", key))
+        arrived(qin.at[xof[key], :, 0:2], ("q", key))
     outs = []
     for j in range(nx):
         outs.append(local(qin.at[j, :, 1], kn_ref.at[j * hx:(j + 1) * hx]))
-        outs.append(local(qin.at[j, :, 2], vn_ref.at[j * hx:(j + 1) * hx]))
-    pos = pos_ref[...]
-    bu_t, bv_t = bu_ref[...].T, bv_ref[...].T
+    for cp in c_bias:
+        cp.wait()
+    pos = posv[...]
+    bu_t, bv_t = bu[...].T, bv[...].T
     scale = 1.0 / math.sqrt(hd)
     selfs, qvs = [], []
     for h in range(n_heads):
@@ -303,6 +308,10 @@
         p_ref[j] = jnp.where(pos == j, 0.0, probs[j])
     p_ref[n_slots] = self_prob
     c_v.wait()
+    for key in "LRO":
+        arrived(qin.at[xof[key], :, 2], ("v", key))
+    for j in range(nx):
+        outs.append(local(qin.at[j, :, 2], vn_ref.at[j * hx:(j + 1) * hx]))
     for h in range(n_heads):
         acc = p_ref[n_slots, h:h + 1, :] * qin[h // hx, h % hx, 2].astype(F32)
         for j in range(n_slots):
@@ -311,11 +320,13 @@
     oall[x] = o_t[...].T.astype(BF16)
     half = rows // 2
 
-    def o_unit(xx, h):
-        return oall.at[xx, h * half:(h + 1) * half]
-
-    x_start("o", o_unit)
-    up_relay(1)
+    oq = rows // 4
+
+    def o_unit(px, k0, n):
+        return oall.at[xof[px], k0 * oq:(k0 + n) * oq]
+
+    for k0, n, to, frm in ((0, 1, right, "L"), (2, 1, left, "R"), (1, 1, right, "L"), (3, 1, left, "R"), (2, 2, right, "L"), (0, 2, left, "R")):
+        send(o_unit("S", k0, n), o_unit("S", k0, n), to, ("o", frm, k0))
     c_wo.wait()
     arrived(wo_land.at[1 - c], "wo")
     wo[...] = jnp.concatenate([wo_land[0], wo_land[1]], axis=1)
@@ -329,16 +340,18 @@
         in1[y, g] = st1[g, y]
 
     out_proj("S")
-    x_relay("o", o_unit, "L")
-    x_relay("o", o_unit, "R")
+    for frm, k, to in (("L", 0, right), ("R", 2, left), ("L", 1, right), ("R", 3, left)):
+        arrived(o_unit(frm, k, 1), ("o", frm, k))
+        send(o_unit(frm, k, 1), o_unit(frm, k, 1), to, ("o", "O", k))
     up_send(2)
-    x_wait("o", o_unit, "L", 1)
+    arrived(o_unit("L", 2, 2), ("o", "L", 2))
     out_proj("L")
-    x_wait("o", o_unit, "R", 0)
+    arrived(o_unit("R", 0, 2), ("o", "R", 0))
     out_proj("R")
-    x_wait("o", o_unit, "O", 0)
-    x_wait("o", o_unit, "O", 1)
+    for k in range(4):
+        arrived(o_unit("O", k, 1), ("o", "O", k))
     out_proj("O")
+    up_relay(1)
     gain_m = jnp.concatenate([gall[2 * x, 1:2, :], gall[2 * x + 1, 1:2, :]], axis=1)
     for px in "SLRO":
         for key in "DUO":
@@ -446,13 +459,16 @@
                 st2[j, h] = blk
                 send(st2.at[j, h], in2.at[y, h], dev(x, c, yof[py]), ("r2y", {"D": "U", "U": "D", "O": "O"}[py], h))
 
-    def y_unit(px, py, h):
-        return yfull.at[yof[py], h * hq:(h + 1) * hq, lanes(dx, xof[px])]
+    def y_unit(px, h):
+        return yfull.at[h * hq:(h + 1) * hq, lanes(dx, xof[px])]
+
+    def y_out(px, py, h):
+        return y_ref.at[yof[py], h * hq:(h + 1) * hq, lanes(dx, xof[px])]
 
     def yy_send(px, h):
-        blk = y_unit(px, "S", h)
         for i, key in ((2, "O"), (1, "D"), (ny - 1, "U")):
-            send(blk, blk, dev(x, c, yp(i)), ("yy", px, h, key))
+            send(y_unit(px, h), y_out(px, "S", h), dev(x, c, yp(i)), ("yy", px, h, key))
+        outs.append(local(y_unit(px, h), y_out(px, "S", h)))
 
     def finish(h):
         for key in "DUO":
@@ -462,13 +478,13 @@
             acc = acc + in2[k, h].astype(F32)
         yst[h] = (hbuf[piece(h), :] + acc).astype(BF16).reshape(nx, hq, dx)
         for i, key in ((2, "O"), (1, "L"), (nx - 1, "R")):
-            send(yst.at[h, xp(i)], y_unit("S", "S", h), dev(xp(i), c, y), ("yx", key, h))
-        yfull[y, h * hq:(h + 1) * hq, lanes(dx, x)] = yst[h, x]
+            send(yst.at[h, xp(i)], y_unit("S", h), dev(xp(i), c, y), ("yx", key, h))
+        yfull[h * hq:(h + 1) * hq, lanes(dx, x)] = yst[h, x]
         yy_send("S", h)
 
     def y_forward(h):
         for px in "LRO":
-            arrived(y_unit(px, "S", h), ("yx", px, h))
+            arrived(y_unit(px, h), ("yx", px, h))
             yy_send(px, h)
 
     xs_direct("mx", m_unit, "S", 0)
@@ -489,14 +505,14 @@
             arrived(wup.at[2 * xof[key] + 1 - c, UP_PARTS[p]:UP_PARTS[p + 1]], ("us", p, key))
     hidden([("S", 0)], xs_direct)
     xs_last("mx", m_unit, "S", 1)
-    ys_send("O", 1)
     xs_near("mx", m_unit, "S", 1)
-    ys_send("L", 1)
-    ys_send("R", 1)
-    hidden([("S", 1)], xs_direct)
+    hidden([("S", 1)])
     for px in "SOLR":
         ys_relay(px, 0)
+    for px in "OLR":
+        ys_send(px, 1)
     hidden([("D", 0), ("U", 0)])
+    xs_relay("z", z_unit, "S", 1)
     ys_last(0)
     hidden([("O", 0)])
     for px in "SLRO":
@@ -507,7 +523,6 @@
     c_dn.wait()
     arrived(wdn.at[1 - c], "dn")
     xs_near("z", z_unit, "S", 0)
-    xs_near("z", z_unit, "S", 1)
     down([("S", 0), ("S", 1)])
     xs_relay("z", z_unit, "O", 0)
     ys_last(1)
@@ -518,16 +533,15 @@
     down([("O", 0)])
     xs_relay("z", z_unit, "O", 1)
     down([("D", 1), ("U", 1)])
+    down([("O", 1)])
     finish(0)
-    down([("O", 1)])
     y_forward(0)
     finish(1)
     y_forward(1)
     for h in range(2):
         for px in "SLRO":
             for key in "DUO":
-                arrived(y_unit(px, key, h), ("yy", px, h, key))
-    outs.append(local(yfull, y_ref))
+                arrived(y_out(px, key, h), ("yy", px, h, key))
     for cp in pending:
         cp.wait_send()
     for cp in outs:
@@ -578,13 +592,17 @@
         fx = ff // nx
         qr = rows // ny
         any_spec = pl.BlockSpec(memory_space=pl.ANY)
-        vmem_spec = pl.BlockSpec(memory_space=pltpu.VMEM)
         vm = pltpu.VMEM
         scratch = [
             vm((nx, rows, d_model), BF16),
             vm((nx * rows, d_model), BF16),
             vm((2, 3 * hx * hd, 2 * rows), F32),
-            vm((2, ds), F32),
+            vm((ds,), F32),
+            vm((ds,), F32),
+            vm((n_slots, dx), BF16),
+            vm((n_heads, hd), F32),
+            vm((n_heads, hd), F32),
+            vm((1, rows), jnp.int32),
             vm((2 * nx, 2, ds), F32),
             vm((1, d_model), F32),
             vm((2, 3, nx, hd, ds), BF16),
@@ -618,7 +636,7 @@
             vm((ny - 1, 2, rows // 2, dx), BF16),
             vm((ny, 2, rows // 2, dx), BF16),
             vm((2, nx, qr // 2, dx), BF16),
-            vm((ny, qr, d_model), BF16),
+            vm((qr, d_model), BF16),
             pltpu.SemaphoreType.DMA((N_REMOTE,)),
             pltpu.SemaphoreType.DMA((N_REMOTE,)),
             pltpu.SemaphoreType.DMA((N_LOCAL,)),
@@ -630,7 +648,7 @@
                 jax.ShapeDtypeStruct((n_heads, hd, rows), BF16),
                 jax.ShapeDtypeStruct((n_heads, hd, rows), BF16),
             ),
-            in_specs=[any_spec, vmem_spec, vmem_spec, any_spec, any_spec, any_spec, any_spec, any_spec, vmem_spec, vmem_spec, vmem_spec, any_spec, any_spec, vmem_spec],
+            in_specs=[any_spec] * 14,
             out_specs=(any_spec, any_spec, any_spec),
             scratch_shapes=scratch,
             compiler_params=pltpu.CompilerParams(collective_id=0, has_side_effects=True, vmem_limit_bytes=60 * 2**20),

time: 119 us -> 113 us (0.950)
  Pallas kernels: 118 us -> 112 us
    pallas_call x1, Pallas kernels: 116 us -> 110 us  [device_step(): pl.pallas_call(functools.partial(layer_kernel, nx, ny), out_shape=(jax.Sh...]
where the time goes in v4:
time: 113 us
  Pallas kernels  112 us (99%)
    pallas_call x1, Pallas kernels, device_step(): pl.pallas_call(functools.partial(layer_kernel, nx, ny), out_shape=(jax.Sh...  110 us

profile of v4, /device:TPU:96, one launch (start us, length us, event | category | flops | bytes accessed | tf_op | source)
XLA Modules:
  0.0 112.9 jit_solution(10420161662753144113)
XLA Ops:
  0.6 110.0 %shard_map.157 = (bf16[4,32,2560]{2,1,0:T(8,128)(2,1)}, bf16[8,80,128]{2,1,0:T(8,128)(2,1)}, bf16[8,80,128]{2,1,0:T(8,128)(2,1)}) custom-call(bf16[128,2560]{1,0:T(8,128)(2,1)} %tok_ref.1, f32[320]{0:T(512)} %ga_ref.1, f32[320]{0:T(512)} %gm_ref.1, bf16[3,4,2,80,320]{4,3,2,1,0:T(8,128)(2,1)} %bitcast.17, bf16[640,320]{1,0:T(8,128)(2,1)} %bitcast.19, ...), custom_call_target="tpu_custom_call" | custom-call | tf_op jit(solution)/shard_map/pallas_call | solution.py:644
  110.7 2.1 %shard_map.158 = (bf16[128,2560]{1,0:T(8,128)(2,1)}, bf16[8,80,128]{2,1,0:T(8,128)(2,1)}, bf16[8,80,128]{2,1,0:T(8,128)(2,1)}) custom-call(bf16[128,2560]{1,0:T(8,128)(2,1)} %bitcast.18, bf16[8,80,128]{2,1,0:T(8,128)(2,1)} %get-tuple-element.10.refs_1_, bf16[8,80,128]{2,1,0:T(8,128)(2,1)} %get-tuple-element.11.refs_2_), custom_call_target="tpu_custom_call" | custom-call | tf_op jit(solution)/shard_map/pallas_call | solution.py:569

commit v5 on v4

--- a/solution.py
+++ b/solution.py
@@ -506,13 +506,12 @@
     hidden([("S", 0)], xs_direct)
     xs_last("mx", m_unit, "S", 1)
     xs_near("mx", m_unit, "S", 1)
-    hidden([("S", 1)])
+    hidden([("S", 1)], xs_direct)
     for px in "SOLR":
         ys_relay(px, 0)
     for px in "OLR":
         ys_send(px, 1)
     hidden([("D", 0), ("U", 0)])
-    xs_relay("z", z_unit, "S", 1)
     ys_last(0)
     hidden([("O", 0)])
     for px in "SLRO":
@@ -523,6 +522,7 @@
     c_dn.wait()
     arrived(wdn.at[1 - c], "dn")
     xs_near("z", z_unit, "S", 0)
+    xs_near("z", z_unit, "S", 1)
     down([("S", 0), ("S", 1)])
     xs_relay("z", z_unit, "O", 0)
     ys_last(1)

time: 113 us -> 113 us (level)
  no operation moved by 1% of the time
where the time goes in v5:
time: 113 us
  Pallas kernels  112 us (99%)
    pallas_call x1, Pallas kernels, device_step(): pl.pallas_call(functools.partial(layer_kernel, nx, ny), out_shape=(jax.Sh...  110 us

profile of v5, /device:TPU:96, one launch (start us, length us, event | category | flops | bytes accessed | tf_op | source)
XLA Modules:
  0.0 112.7 jit_solution(2438316896681075048)
XLA Ops:
  0.6 109.8 %shard_map.157 = (bf16[4,32,2560]{2,1,0:T(8,128)(2,1)}, bf16[8,80,128]{2,1,0:T(8,128)(2,1)}, bf16[8,80,128]{2,1,0:T(8,128)(2,1)}) custom-call(bf16[128,2560]{1,0:T(8,128)(2,1)} %tok_ref.1, f32[320]{0:T(512)} %ga_ref.1, f32[320]{0:T(512)} %gm_ref.1, bf16[3,4,2,80,320]{4,3,2,1,0:T(8,128)(2,1)} %bitcast.17, bf16[640,320]{1,0:T(8,128)(2,1)} %bitcast.19, ...), custom_call_target="tpu_custom_call" | custom-call | tf_op jit(solution)/shard_map/pallas_call | solution.py:644
  110.4 2.1 %shard_map.158 = (bf16[128,2560]{1,0:T(8,128)(2,1)}, bf16[8,80,128]{2,1,0:T(8,128)(2,1)}, bf16[8,80,128]{2,1,0:T(8,128)(2,1)}) custom-call(bf16[128,2560]{1,0:T(8,128)(2,1)} %bitcast.18, bf16[8,80,128]{2,1,0:T(8,128)(2,1)} %get-tuple-element.10.refs_1_, bf16[8,80,128]{2,1,0:T(8,128)(2,1)} %get-tuple-element.11.refs_2_), custom_call_target="tpu_custom_call" | custom-call | tf_op jit(solution)/shard_map/pallas_call | solution.py:569
